TPU v7x, 32 devices: a whole 2x2x4 slice. The times are simulated.
32 devices in a mesh: rep: 1, dp: 32 (over x, y, z, core).
Axes of the slice: x: 2, y: 2, z: 4, core: 2. Of those that a mesh axis runs over, the one named last changes fastest.
Arguments:
- g_w_gate: bfloat16 [32, 2, 1152, 4608], P(('rep', 'dp'))
- g_w_up: bfloat16 [32, 2, 1152, 4608], P(('rep', 'dp'))
- g_w_down: bfloat16 [32, 2, 4608, 1152], P(('rep', 'dp'))
- w_gate: bfloat16 [2, 1152, 4608], replicated
- w_up: bfloat16 [2, 1152, 4608], replicated
- w_down: bfloat16 [2, 4608, 1152], replicated
- m_w_gate: float32 [2, 1152, 4608], P(None, 'dp')
- m_w_up: float32 [2, 1152, 4608], P(None, 'dp')
- m_w_down: float32 [2, 4608, 1152], P(None, 'dp')
- v_w_gate: float32 [2, 1152, 4608], P(None, 'dp')
- v_w_up: float32 [2, 1152, 4608], P(None, 'dp')
- v_w_down: float32 [2, 4608, 1152], P(None, 'dp')
Outputs:
- output 1: bfloat16 [2, 1152, 4608], P('rep')
- output 2: bfloat16 [2, 1152, 4608], P('rep')
- output 3: bfloat16 [2, 4608, 1152], P('rep')
- output 4: float32 [2, 1152, 4608], P('rep', 'dp')
- output 5: float32 [2, 1152, 4608], P('rep', 'dp')
- output 6: float32 [2, 4608, 1152], P('rep', 'dp')
- output 7: float32 [2, 1152, 4608], P('rep', 'dp')
- output 8: float32 [2, 1152, 4608], P('rep', 'dp')
- output 9: float32 [2, 4608, 1152], P('rep', 'dp')
All inputs are finite; a program needn't handle non-finite values.
Results may differ from a plain program's by a relative error of at most 0.022.
Values are sent between devices in bfloat16 or wider.
A program may use at most 2 GiB of HBM per device.

v0:
```python
import jax
import jax.numpy as jnp
from jax import lax
from jax.sharding import PartitionSpec as P


def adamw(w, m, v, g):
    m = 0.9 * m + 0.1 * g
    v = 0.95 * v + 0.05 * g * g
    step = m * lax.rsqrt(v + 1e-8) + 0.1 * w
    return (w - 0.02 * step).astype(jnp.bfloat16), m, v


def clipped(gradients, sum_of_squares, count):
    factor = jnp.minimum(1.0, 0.5 * lax.rsqrt(sum_of_squares / count + 1e-30))
    return [g * factor for g in gradients]


def solution(mesh):
    def step(*arrays):
        terms, weights, m, v = (arrays[i : i + 3] for i in (0, 3, 6, 9))
        gradients = [lax.psum_scatter(t[0], "dp", scatter_dimension=1, tiled=True).astype(jnp.float32) for t in terms]
        squares = lax.psum(sum(jnp.sum(g * g) for g in gradients), "dp")
        gradients = clipped(gradients, squares, lax.psum(1, "dp") * sum(g.size for g in gradients))
        me = lax.axis_index("dp")
        own = [lax.dynamic_slice_in_dim(w, me * one.shape[1], one.shape[1], 1).astype(jnp.float32) for w, one in zip(weights, m, strict=True)]
        new = [adamw(w, m, v, g) for w, m, v, g in zip(own, m, v, gradients, strict=True)]
        whole = [lax.all_gather(one[0], "dp", axis=1, tiled=True) for one in new]
        return (*whole, *(one[1] for one in new), *(one[2] for one in new))

    all_of, cut = P(None, None, None), P(None, "dp", None)
    return jax.shard_map(
        step,
        mesh=mesh,
        in_specs=(P(("rep", "dp"), None, None, None),) * 3 + (all_of,) * 3 + (cut,) * 6,
        out_specs=(P("rep", None, None),) * 3 + (P("rep", "dp", None),) * 6,
        check_vma=False,
    )
```

profile of v0, /device:TPU:0, one launch (start us, length us, event | category | flops | bytes accessed | tf_op | source)
XLA Modules:
  0.0 1503.1 jit_solution(14828343885298961460)
XLA Ops:
  7.2 0.0 all-reduce.5.cloned.1.call-start
  7.2 94.4 %copy.40 = bf16[1,2,1152,4608]{3,1,2,0:T(2,128)(2,1)} copy(bf16[1,2,1152,4608]{3,2,1,0:T(8,128)(2,1)} %param.12) | data formatting | bytes 42467328 | tf_op args[0]
  101.7 0.0 all-reduce.5.cloned.1.call-update
  101.7 0.0 all-reduce.7.cloned.1.call-start
  101.7 94.4 %copy.39 = bf16[1,2,1152,4608]{3,1,2,0:T(2,128)(2,1)} copy(bf16[1,2,1152,4608]{3,2,1,0:T(8,128)(2,1)} %param.13) | data formatting | bytes 42467328 | tf_op args[1]
  196.2 0.0 all-reduce.7.cloned.1.call-update
  196.2 0.0 reduce-scatter.2.cloned.1.call-start
  196.3 0.7 reduce-scatter.2.cloned.1.call-update
  196.9 0.0 all-gather.4.cloned.1.call-start
  197.0 250.7 %all-reduce.5.cloned.1.call-done = bf16[2,1152,4608]{2,0,1:T(2,128)(2,1)} async-done(((bf16[2,1152,4608]{2,0,1:T(2,128)(2,1)}), bf16[2,1152,4608]{2,0,1:T(2,128)(2,1)}) %all-reduce.5.cloned.1.call-update) | async-done | bytes 21233680
  447.7 3.1 fusion.8
  450.8 346.3 %all-reduce.7.cloned.1.call-done = bf16[2,1152,4608]{2,0,1:T(2,128)(2,1)} async-done(((bf16[2,1152,4608]{2,0,1:T(2,128)(2,1)}), bf16[2,1152,4608]{2,0,1:T(2,128)(2,1)}) %all-reduce.7.cloned.1.call-update) | async-done | bytes 21233680
  797.0 3.1 fusion.9
  801.4 219.3 %reduce-scatter.2.cloned.1.call-done = bf16[2,144,1152]{2,1,0:T(8,128)(2,1)} async-done(((bf16[2,4608,1152]{2,1,0:T(8,128)(2,1)}), bf16[2,144,1152]{2,1,0:T(8,128)(2,1)}) %reduce-scatter.2.cloned.1.call-update) | async-done | bytes 663568 | tf_op jit(solution)/shard_map/reduce_scatter | solution.py:22
  1020.7 2.0 fusion.10
  1023.4 1.4 constant_dynamic-slice_fusion.1
  1024.7 39.6 %psum.7 = f32[]{:T(128)} all-reduce(f32[]{:T(128)S(6)} %add.65), channel_id=1, replica_groups=mesh['rep'=1,'dp'=32] {'dp'}, use_global_device_ids=true, to_apply=%region_6.0 | all-reduce | flops 1 | bytes 8 | tf_op jit(solution)/shard_map/psum | solution.py:23
  1065.1 6.1 fusion.19
  1071.2 0.0 all-gather.4.cloned.1.call-update
  1071.2 0.2 all-gather.6.cloned.1.call-start
  1071.5 1.4 constant_dynamic-slice_fusion
  1072.8 7.3 fusion.20
  1080.1 0.0 all-gather.6.cloned.1.call-update
  1080.1 0.0 all-gather.8.cloned.1.call-start
  1080.2 3.2 fusion.15
  1083.5 0.0 all-gather.8.cloned.1.call-update
  1083.5 122.3 %all-gather.4.cloned.1.call-done = bf16[2,1152,4608]{2,0,1:T(2,128)(2,1)} async-done(((bf16[2,36,4608]{2,0,1:T(2,128)(2,1)}), bf16[2,1152,4608]{2,0,1:T(2,128)(2,1)}) %all-gather.4.cloned.1.call-update) | async-done | bytes 21233680 | tf_op jit(solution)/shard_map/all_gather | solution.py:28
  1205.8 19.5 %copy.31 = bf16[2,1152,4608]{2,1,0:T(8,128)(2,1)} copy(bf16[2,1152,4608]{2,0,1:T(2,128)(2,1)} %all-gather.4.cloned.1.call-done) | data formatting | bytes 42467328
  1225.3 117.3 %all-gather.6.cloned.1.call-done = bf16[2,1152,4608]{2,0,1:T(2,128)(2,1)} async-done(((bf16[2,36,4608]{2,0,1:T(2,128)(2,1)}), bf16[2,1152,4608]{2,0,1:T(2,128)(2,1)}) %all-gather.6.cloned.1.call-update) | async-done | bytes 21233680 | tf_op jit(solution)/shard_map/all_gather | solution.py:28
  1342.6 19.5 %copy.32 = bf16[2,1152,4608]{2,1,0:T(8,128)(2,1)} copy(bf16[2,1152,4608]{2,0,1:T(2,128)(2,1)} %all-gather.6.cloned.1.call-done) | data formatting | bytes 42467328
  1362.1 116.7 %all-gather.8.cloned.1.call-done = bf16[2,4608,1152]{2,1,0:T(8,128)(2,1)} async-done(((bf16[2,144,1152]{2,1,0:T(8,128)(2,1)}), bf16[2,4608,1152]{2,1,0:T(8,128)(2,1)}) %all-gather.8.cloned.1.call-update) | async-done | bytes 21233680 | tf_op jit(solution)/shard_map/all_gather | solution.py:28
  1478.9 17.4 %copy.44 = bf16[2,4608,1152]{2,1,0:T(8,128)(2,1)} copy(bf16[2,4608,1152]{2,1,0:T(8,128)(2,1)} %all-gather.8.cloned.1.call-done) | data formatting | bytes 42467328
  (10 shorter events, 0.0 us)
Async XLA Ops:
  7.2 440.5 %all-reduce.5.cloned.1.call-start = ((), (), s32[]{:S(2)}) async-start(), calls=%async_computation.5 | async-start | bytes 42467328
  101.7 695.4 %all-reduce.7.cloned.1.call-start = ((), (), s32[]{:S(2)}) async-start(), calls=%async_computation.6 | async-start | bytes 42467328
  196.2 824.5 %reduce-scatter.2.cloned.1.call-start = ((), (), s32[]{:S(2)}) async-start(), calls=%async_computation.1 | async-start | bytes 21897216 | tf_op jit(solution)/shard_map/reduce_scatter | solution.py:22
  196.9 1008.8 %all-gather.4.cloned.1.call-start = ((), (), s32[]{:S(2)}) async-start(), calls=%async_computation.2 | async-start | bytes 21897216 | tf_op jit(solution)/shard_map/all_gather | solution.py:28
  450.8 614.3 %copy-start.3 = (f32[2,36,4608]{2,0,1:T(2,128)S(1)}, f32[2,36,4608]{2,0,1:T(2,128)}, u32[]{:S(2)}) copy-start(f32[2,36,4608]{2,0,1:T(2,128)} %param.21) | copy-start | bytes 3981316
  450.8 614.3 %copy-start.4 = (f32[2,36,4608]{2,0,1:T(2,128)S(1)}, f32[2,36,4608]{2,0,1:T(2,128)}, u32[]{:S(2)}) copy-start(f32[2,36,4608]{2,0,1:T(2,128)} %param.18) | copy-start | bytes 3981316
  1071.2 271.4 %all-gather.6.cloned.1.call-start = ((), (), s32[]{:S(2)}) async-start(), calls=%async_computation.3 | async-start | bytes 21897216 | tf_op jit(solution)/shard_map/all_gather | solution.py:28
  1072.8 7.4 copy-start
  1072.8 7.4 copy-start.1
  1072.8 7.4 copy-start.2
  1080.1 398.7 %all-gather.8.cloned.1.call-start = ((), (), s32[]{:S(2)}) async-start(), calls=%async_computation.4 | async-start | bytes 21897216 | tf_op jit(solution)/shard_map/all_gather | solution.py:28
Sparse Core Ops, SparseCore 0:
  101.8 345.8 all-reduce.4
  454.7 342.2 all-reduce.6
  803.5 217.1 reduce-scatter.1
  1071.3 134.4 all-gather.3
  1209.3 133.3 all-gather.5
  1345.5 133.2 all-gather.7
where the time goes:
time: 1500 us
  waiting for transfers between devices  1170 us (78%)
  local copies, waits for them, and re-layouts  248 us (17%)
  blocking collectives  39.6 us (3%)
  other arithmetic  24.8 us (2%)
  between operations  16.9 us (1%)
    unnamed x8, waiting for transfers between devices  598 us
    all_gather x3, waiting for transfers between devices, step(): whole = [lax.all_gather(one[0], 'dp', axis=1, tiled=True) for one in new]  356 us
    unnamed x15, local copies, waits for them, and re-layouts  245 us
    reduce_scatter x1, waiting for transfers between devices, step(): lax.psum_scatter(t[0], 'dp', scatter_dimension=1, tiled=True)  219 us
    psum x1, blocking collectives, step(): squares = lax.psum(sum((jnp.sum(g * g) for g in gradients)), 'dp')  39.6 us
  transfers between devices with their start and end apart: 6, of which 6 were waited for; matrix products, arithmetic and copies ran while one was open for 10% of the time, Pallas kernels for 0%

commit v1 on v0

v1 whole, which is shorter than its diff:
```python
import functools

import jax
import jax.numpy as jnp
from jax import lax
from jax.experimental import pallas as pl
from jax.experimental.pallas import tpu as pltpu
from jax.sharding import PartitionSpec as P

MESH = pl.DeviceIdType.MESH
BF, F32 = jnp.bfloat16, jnp.float32
DMA = pltpu.SemaphoreType.DMA
VMEM, HBM = pltpu.VMEM, pltpu.HBM
ALL = slice(None)
L, X, Y, Z, U, CORES = 2, 2, 2, 4, 9, 2
N = X * Y * Z * CORES
SUB, ROWS, LANES = 8, 16, 128
T3 = (U, ROWS, LANES)
NP = 3 * L
HALF = NP - L
OWN = 5
PART = {'A': pl.ds(0, OWN), 'B': pl.ds(OWN, 3), 'C': U - 1}
VM, HB, ANY = (pl.BlockSpec(memory_space=s) for s in (VMEM, HBM, pl.ANY))


def tiled(a):
    l, r, c = a.shape
    return a.reshape(l, r // SUB, SUB, c // LANES, LANES).swapaxes(2, 3)


def untiled(a, r, c):
    return a.reshape(L, r // SUB, c // LANES, SUB, LANES).swapaxes(2, 3).reshape(L, r, c)


def view_gu(g): return tiled(g).reshape(L, X, Y, Z, U, CORES, *T3)
def view_d(g): return tiled(g).reshape(L, X, Y, Z, CORES, U, *T3)


def place():
    d = lax.axis_index("dp")
    d, c = d // CORES, d % CORES
    d, z = d // Z, d % Z
    return d // Y, d % Y, z, c


def dev(x, y, z, c): return 0, ((x * Y + y) * Z + z) * CORES + c


def line(z):
    h = z // 2
    return (z == 1) | (z == 2), [z, 1 - z + Z * h, 2 - h, 3 - 3 * h], z + 1 - 2 * h, 3 * h


def over(n, f): lax.fori_loop(0, n, lambda i, _: (f(i), 0)[1], 0)


def copy(src, dst, sem): return pltpu.make_async_copy(src, dst, sem)


def remote(src, dst, ss, rs, to): return pltpu.make_async_remote_copy(src, dst, ss, rs, device_id=to, device_id_type=MESH)


def got(ref, sem): copy(ref, ref, sem).wait()


def split(name): return name[0], name[1], int(name[-1]) if name[-1].isdigit() else 0


def lagged(names): return [(n.rstrip('+'), n.count('+')) for n in names]


RS_ORDER = ['By0', 'Ax0', 'Ax7+', 'Cz0', 'By2', 'Bf++', 'Az1+', 'Ax1', 'Ax4', 'Cz1', 'By1', 'Ax2', 'Cz2', 'Ax6', 'Ax5', 'Bx+', 'Ay0', 'Bz0', 'Ay1', 'Bz2', 'Ax3', 'By3', 'Bz1', 'Ay2', 'Az0', 'Cx', 'Ay3+', 'Az2+', 'Af++', 'Cf++', 'Cy+']
TURN = 24
CLASSES = {
    'A': ((OWN,), ['Ax0', 'Ax1', 'Ax2', 'Ax3', 'Ax4', 'Ax5', 'Ax6', 'Ax7', 'Ay0', 'Ay1', 'Ay2', 'Ay3', 'Az0', 'Az1', 'Az2', 'Af']),
    'By': ((X, 3), ['By0', 'By1', 'By2', 'By3', 'Bz0', 'Bz1', 'Bz2']),
    'Bx': ((3,), ['Bx', 'Bf']),
    'Cz': ((X, Y), ['Cz0', 'Cz1', 'Cz2']),
    'Cx': ((Y,), ['Cx']),
    'Cy': ((), ['Cy', 'Cf']),
}
CLASS_OF = {n: (k, i) for k, (_, names) in CLASSES.items() for i, n in enumerate(names)}
ARRIVE = {'Ax': (8, 'A'), 'Ay': (Z, 'A'), 'Az': (5, 'A'), 'By': (Z, 'By'), 'Bz': (5, 'By'), 'Bx': (1, 'Bx'), 'Cz': (5, 'Cz'), 'Cx': (1, 'Cx'), 'Cy': (1, 'Cy')}
LAST, CROSS = 2, 4


def rs_kernel(order, gg, gu, gd, Ggu, Gd, TOT, PARTNER, *scr):
    scr = iter(scr)
    take = lambda names: {n: next(scr) for n in names}
    own, par, snd, rcv = take(CLASSES), take(CLASSES), take(CLASSES), take(ARRIVE)
    fin, gx, acc, sall = take(range(4)).values()
    own_s, par_s, snd_s, first_s, rcv_s = take(CLASSES), take(CLASSES), take(CLASSES), take(CLASSES), take(ARRIVE)
    d2d_ss, d2d_rs, gx_ss, gx_rs, sa_ss, sa_rs = take(range(6)).values()
    x, y, z, c = place()
    ox, oy, oc = 1 - x, 1 - y, 1 - c
    me = lax.axis_index("dp")
    mid, near, inner, _ = line(z)
    zo = near[::-1]
    side = z + 1 - 2 * (z % 2)
    NX, NY, NC = dev(ox, y, z, c), dev(x, oy, z, c), dev(x, y, z, oc)

    def block(name):
        n, axis, i = split(name)
        u = PART[n]
        if axis == 'f': return x, y, z, u
        if n == 'A':
            if axis == 'x': return ox, (oy if i < Z else y), zo[i % Z], u
            return x, (oy if axis == 'y' else y), zo[i], u
        if n == 'B':
            if axis == 'x': return ox, y, z, u
            return ALL, (oy if axis == 'y' else y), zo[i], u
        return {'z': (ALL, ALL, zo[i], u), 'x': (ox, ALL, z, u), 'y': (x, oy, z, u)}[axis]

    def cut(k, l, b, core):
        return gd.at[(l, *b[:3], core, b[3])] if k == 2 else (gg, gu)[k].at[(l, *b, core)]

    def reload(name, p):
        cl, i = CLASS_OF[name]
        b = block(name)
        @pl.when((p >= 0) & (p < NP))
        def _():
            for k in range(3):
                @pl.when(p // L == k)
                def _(): copy(cut(k, p % L, b, c), own[cl].at[i], own_s[cl].at[i]).start()
            @pl.when(p > 0)
            def _(): copy(PARTNER.at[(p, *b)], par[cl].at[i], par_s[cl].at[i]).start()

    def send(name, p):
        cl, i = CLASS_OF[name]
        n, axis, j = split(name)
        if axis == 'x': to, slot = NX, j
        elif axis == 'y': to, slot = NY, j
        elif j < 2: to, slot = dev(x, y, inner, c), j + 3 * mid.astype(jnp.int32)
        else: to, slot = dev(x, y, side, c), LAST
        kind = name[:2]
        return remote(snd[cl].at[i], rcv[kind].at[p, slot], snd_s[cl].at[i], rcv_s[kind].at[p, slot], to)

    def add(dst, refs, lead, last):
        def one(*idx):
            at = idx if idx else ...
            t = sum(r[at].astype(F32) for r in refs).astype(BF)
            dst[at] = t
            if last:
                t = t.astype(F32)
                acc[...] += jnp.sum(t * t, axis=0)
        if not lead: one()
        elif len(lead) == 1: over(lead[0], one)
        else: over(lead[0], lambda i: over(lead[1], lambda j: one(i, j)))

    def task(name, p):
        cl, i = CLASS_OF[name]
        n, axis, j = split(name)
        lead = CLASSES[cl][0]
        R = lambda kind, s: rcv[kind].at[p, s]
        def arrive(*which):
            for kind, s in which: got(R(kind, s), rcv_s[kind].at[p, s])
        got(own[cl].at[i], own_s[cl].at[i])
        got(par[cl].at[i], par_s[cl].at[i])
        zk, refs, far, wait, farwait = n + 'z', [], [], [], []
        if axis == 'z':
            s = (0, 1, 3)[j]
            far, farwait = [R(zk, s)], [(zk, s)]
            wait = {'A': [('Ax', Z + j), ('Ay', j)], 'B': [('By', j)], 'C': []}[n]
            refs = [R(*w) for w in wait]
        elif name[:2] == 'Ay':
            wait = [('Ax', j)]
            refs = [R(*w) for w in wait]
        elif name == 'Af':
            wait, farwait = [('Ax', Z + 3), ('Ay', 3), (zk, LAST)], [(zk, CROSS)]
            refs, far = [R(*w) for w in wait], [R(zk, CROSS)]
        elif axis != 'y' or n == 'C':
            if n == 'B' and axis == 'x' or n == 'C' and axis == 'x': wait, farwait = [(zk, LAST)], [(zk, CROSS)]
            if name == 'Bx': wait += [('By', 3)]
            if name in ('Bf', 'Cy'): wait = [(n + 'x', 0)]
            if name == 'Cf': wait = [('Cy', 0)]
            here = {'Bx': (ox,), 'Bf': (x,), 'Cx': (ox,), 'Cy': (x, oy), 'Cf': (x, y)}.get(name)
            if here:
                refs, far = [R(zk, LAST).at[here]], [R(zk, CROSS).at[here]]
                if n == 'B': refs += [R('By', 3).at[here]]
                if name == 'Bf': refs += [R('Bx', 0)]
                if name == 'Cy': refs += [R('Cx', 0).at[oy]]
                if name == 'Cf': refs += [R('Cx', 0).at[y], R('Cy', 0)]
        arrive(*wait)
        last = axis == 'f'
        if last: dst = fin.at[p, PART[n]]
        else:
            @pl.when(p > 0)
            def _(): send(name, p).wait_send()
            dst = snd[cl].at[i]
        refs = [own[cl].at[i], par[cl].at[i]] + refs
        if far:
            @pl.when(mid)
            def _():
                arrive(*farwait)
                add(dst, refs + far, lead, last)
            @pl.when(jnp.logical_not(mid))
            def _(): add(dst, refs, lead, last)
        else: add(dst, refs, lead, last)
        if not last: send(name, p).start()

    def swap0(name):
        cl, i = CLASS_OF[name]
        return remote(cut(0, 0, block(name), oc), par[cl].at[i], first_s[cl].at[i], par_s[cl].at[i], NC)

    def swap(p):
        parts = [(ox, ALL, ALL, PART['A']), (ALL, ALL, ALL, PART['B']), (ALL, ALL, ALL, PART['C']), (x, ALL, ALL, PART['A'])]
        return [remote(cut(p // L, p % L, q, oc), PARTNER.at[(p, *q)], d2d_ss.at[p, i], d2d_rs.at[p, i], NC) for i, q in enumerate(parts)]

    acc[...] = jnp.zeros_like(acc)
    for n, _ in order: reload(n, jnp.int32(0))
    b = pltpu.get_barrier_semaphore()
    def others(f):
        def one(i):
            @pl.when(i != me)
            def _(): f((0, i))
        over(N, one)
    others(lambda to: pl.semaphore_signal(b, 1, device_id=to, device_id_type=MESH))
    pl.semaphore_wait(b, N - 1)
    for n, _ in sorted(order, key=lambda t: t[1]): swap0(n).start()
    for p in range(1, NP):
        for cp in swap(p): cp.start()

    finlag = max(lag for n, lag in order if n[1] == 'f')
    def rows(p): return remote(fin.at[p, pl.ds(Z * oc, OWN)], gx.at[p], gx_ss.at[p], gx_rs.at[p], NC)
    def round_(r):
        for i, (n, lag) in enumerate(order):
            p = r - lag
            @pl.when((p >= 0) & (p < NP))
            def _(): task(n, p)
            if i == TURN:
                for q in range(1, NP):
                    @pl.when(q == r + 1)
                    def _():
                        for cp in swap(q): cp.wait_recv()
                for m, ml in order[:TURN]:
                    @pl.when(r >= ml)
                    def _(): reload(m, r - ml + 1)
            if i >= TURN:
                @pl.when(p >= 0)
                def _(): reload(n, p + 1)
        q = r - finlag
        @pl.when((q >= 0) & (q < HALF))
        def _(): rows(q).start()
    over(NP + max(lag for _, lag in order), round_)

    sall[me] = acc[0:SUB] + acc[SUB:ROWS]
    others(lambda to: remote(sall.at[me], sall.at[me], sa_ss, sa_rs, to).start())
    for l in range(L): Gd[l] = fin[HALF + l]
    for p in range(HALF):
        k, l = p // L, p % L
        Ggu[k, l, :, c] = fin[p, pl.ds(Z * c, OWN)]
        rows(p).wait()
        Ggu[k, l, :, oc] = gx[p]
    for n, lag in order:
        swap0(n).wait_send()
        if n[1] != 'f': send(n, NP - 1).wait_send()
    for p in range(1, NP):
        for cp in swap(p): cp.wait_send()
    rest = sall.at[pl.ds(0, N - 1)]
    got(rest, sa_rs)
    got(rest, sa_ss)
    TOT[...] = jnp.sum(sall[...], axis=0)


def rs_call(gg, gu, gd):
    bufs = [VMEM((len(names), *shape, *T3), BF) for shape, names in CLASSES.values()]
    sems = [DMA((len(names),)) for _, names in CLASSES.values()]
    scratch = bufs * 3 + [VMEM((NP, n, *CLASSES[cl][0], *T3), BF) for n, cl in ARRIVE.values()]
    scratch += [VMEM((NP, U, *T3), BF), VMEM((HALF, OWN, *T3), BF), VMEM((ROWS, LANES), F32), VMEM((N, SUB, LANES), F32)]
    scratch += sems * 4 + [DMA((NP, n)) for n, _ in ARRIVE.values()]
    scratch += [DMA((NP, 4)), DMA((NP, 4)), DMA((HALF,)), DMA((HALF,)), DMA(()), DMA(())]
    return pl.pallas_call(
        functools.partial(rs_kernel, lagged(RS_ORDER)),
        out_shape=(VMEM((2, L, OWN, CORES, *T3), BF), VMEM((L, U, *T3), BF), VMEM((SUB, LANES), F32), HBM((NP, X, Y, Z, U, *T3), BF)),
        in_specs=[ANY] * 3,
        out_specs=(VM, VM, VM, HB),
        scratch_shapes=scratch,
        compiler_params=pltpu.CompilerParams(collective_id=0, has_side_effects=True, vmem_limit_bytes=58 * 2**20),
        name="reduce_scatter",
    )(view_gu(gg), view_gu(gu), view_d(gd))


BLOCK, TILES = 36, 36
RUN = TILES * L


def up_kernel(count, Ggu, Gd, TOT, wg, wu, wd, *refs):
    moments, (Wgu, Wd), new, scr = refs[:6], refs[6:8], refs[8:14], refs[14:]
    mom, dm, dv, wb, wdb, ld, st = scr
    x, y, z, c = place()
    loads, stores = [], []
    def start(kept, sems, src, dst):
        kept.append(copy(src, dst, sems.at[len(kept)]))
        kept[-1].start()
    load, store = functools.partial(start, loads, ld), functools.partial(start, stores, st)
    rows = pl.ds(Z, BLOCK)
    load(moments[2], dm)
    load(moments[5], dv)
    load(wd.at[:, x, y, z, c], wdb)
    for k in range(2):
        for i in range(2): load(moments[k + 3 * i], mom.at[k, i, rows])
        load((wg, wu)[k].at[:, x, y, z, pl.ds(Z * c, OWN)], wb.at[k])
    for k in range(2):
        for i in range(2):
            for at in (0, Z + BLOCK): mom[k, i, at:at + Z] = jnp.zeros((Z, TILES, L, LANES), F32)
    s = jnp.sum(jnp.sum(TOT[...], axis=0, keepdims=True), axis=1, keepdims=True)
    factor = jnp.minimum(1.0, 0.5 * lax.rsqrt(s * (1.0 / count) + 1e-30))
    def adamw(w, m, v, g):
        g = g * factor
        m = 0.9 * m + 0.1 * g
        v = 0.95 * v + 0.05 * g * g
        return w - 0.02 * (m * lax.rsqrt(v + 1e-8) + 0.1 * w), m, v
    for cp in loads[:3]: cp.wait()
    def down(l):
        def unit(u):
            for j in range(U):
                at = (l, u, j)
                w, dm[at], dv[at] = adamw(wdb[at].astype(F32), dm[at], dv[at], Gd[at].astype(F32))
                wdb[at] = w.astype(BF)
        over(U, unit)
    over(L, down)
    store(wdb, Wd)
    store(dm, new[2])
    store(dv, new[5])
    for k in range(2):
        for cp in loads[3 + 3 * k:][:3]: cp.wait()
        M, V = (mom.at[k, i].reshape((BLOCK + 2 * Z) * RUN, LANES) for i in range(2))
        def tile(l, u, ch):
            base = (SUB * u + Z - Z * c) * RUN + TILES * ch + l
            for j in range(U):
                g, w = Ggu[k, l, u, ch, j].astype(F32), wb[k, l, u, ch, j].astype(F32)
                half = []
                for e in range(2):
                    at = pl.ds(base + (2 * j + e) * L, SUB, stride=RUN)
                    h = slice(SUB * e, SUB * e + SUB)
                    wn, M[at, :], V[at, :] = adamw(w[h], M[at, :], V[at, :], g[h])
                    half.append(wn)
                wb[k, l, u, ch, j] = jnp.concatenate(half).astype(BF)
        over(L, lambda l: over(OWN, lambda u: over(CORES, lambda ch: tile(l, u, ch))))
        store(wb.at[k], Wgu.at[pl.ds(L * k, L)])
        for i in range(2): store(mom.at[k, i, rows], new[k + 3 * i])
    for cp in stores: cp.wait()


def view_m(m): return m.reshape(L, BLOCK, TILES, LANES).transpose(1, 2, 0, 3)
def unview_m(m): return m.transpose(2, 0, 1, 3).reshape(L, BLOCK, TILES * LANES)
def view_md(m): return tiled(m).reshape(L, U, *T3)


def up_call(Ggu, Gd, total, weights, m, v):
    moments = [f(a) for a, f in zip((*m, *v), (view_m, view_m, view_md) * 2)]
    count = sum(w.size for w in weights)
    down = VMEM((L, U, *T3), F32)
    res = pl.pallas_call(
        functools.partial(up_kernel, count),
        out_shape=(HBM((HALF, OWN, CORES, *T3), BF), HBM((L, U, *T3), BF), *(HBM(a.shape, F32) for a in moments)),
        in_specs=[VM] * 3 + [HB] * 9,
        out_specs=(HB,) * 8,
        scratch_shapes=[VMEM((2, 2, BLOCK + 2 * Z, TILES, L, LANES), F32), down, down, VMEM((2, L, OWN, CORES, *T3), BF), VMEM((L, U, *T3), BF), DMA((9,)), DMA((9,))],
        compiler_params=pltpu.CompilerParams(vmem_limit_bytes=20 * 2**20),
        name="update",
    )(
        *(pltpu.with_memory_space_constraint(a, VMEM) for a in (Ggu, Gd, total)),
        *(pltpu.with_memory_space_constraint(a, HBM) for a in (view_gu(weights[0]), view_gu(weights[1]), view_d(weights[2]), *moments)),
    )
    unview = (unview_m, unview_m, lambda a: untiled(a, *m[2].shape[1:]))
    new = [f(a) for a, f in zip(res[2:], unview * 2)]
    return res[0], res[1], new[:3], new[3:]


AG_ORDER = ['Ax0_1+', 'Ax1_3++', 'By_0+', 'Cz_1+', 'Bo', 'Ay_2+', 'Co', 'Ao', 'Bz_2+', 'Ax0_2+', 'Ay_3+', 'Bx', 'Cy', 'By_1+', 'Cz_2+', 'Ax0_3+', 'Az_1', 'By_3+', 'Ax1_0+', 'Ay_0', 'Az_2', 'Cz_3+', 'Bz_1', 'Ax1_2+', 'Cx', 'Ay_1', 'Ax0_0+', 'By_2++', 'Az_3', 'Bz_3', 'Ax1_1+']


def ag_kernel(order, wgu, wd, VO, tmp, own_s, ex_ss, ex_rs, xs, ys, zis, zos, ds, dr, axr, ayr, azr, byr, bzr, bxr, czr, cxr, cyr):
    x, y, z, c = place()
    ox, oy, oc = 1 - x, 1 - y, 1 - c
    mid, sl, inner, end = line(z)
    NX, NY, NC, ZI, ZO = dev(ox, y, z, c), dev(x, oy, z, c), dev(x, y, z, oc), dev(x, y, inner, c), dev(x, y, end, c)
    zr = {'A': azr, 'B': bzr, 'C': czr}

    def task(name, p):
        n, axis, i = split(name)
        zz = sl[i]
        def at(idx): return VO.at[(p, *idx, PART[n], c)]
        def push(idx, to, ss, rs): remote(at(idx), at(idx), ss.at[p], rs, to).start()
        def give(idx): push(idx, NC, ds, dr.at[p])
        def chain(idx):
            rs = zr[n].at[p, zz]
            if i == 0: push(idx, ZI, zis, rs)
            @pl.when(mid)
            def _():
                if i == 1: push(idx, ZI, zis, rs)
                else: push(idx, ZO, zos, rs)
        if axis == 'o':
            here = x, y, z
            if n == 'A':
                chain(here)
                push(here, NY, ys, ayr.at[p, z])
                push(here, NX, xs, axr.at[p, z, 0])
            elif n == 'B': push(here, NX, xs, bxr.at[p])
            else: push(here, NY, ys, cyr.at[p])
            give(here)
        elif n == 'A':
            if axis == 'z':
                here = x, y, zz
                got(at(here), azr.at[p, zz])
                chain(here)
                push(here, NY, ys, ayr.at[p, zz])
                push(here, NX, xs, axr.at[p, zz, 0])
            elif axis == 'y':
                here = x, oy, zz
                got(at(here), ayr.at[p, zz])
                push(here, NX, xs, axr.at[p, zz, 1])
            else:
                k = int(name[2])
                here = ox, (oy if k else y), zz
                got(at(here), axr.at[p, zz, k])
            give(here)
        elif n == 'B':
            here, wide = (ox, y, z), (ALL, y, zz)
            if axis == 'y':
                here = ALL, oy, zz
                got(at(here), byr.at[p, zz])
            else:
                if axis == 'x': got(at(here), bxr.at[p])
                else:
                    here = wide
                    got(at(here), bzr.at[p, zz])
                chain(wide)
                push(wide, NY, ys, byr.at[p, zz])
            give(here)
        elif axis == 'y':
            here = x, oy, z
            got(at(here), cyr.at[p])
            push((x, ALL, z), NX, xs, cxr.at[p])
            give(here)
        else:
            here, wide = (ox, ALL, z), (ALL, ALL, zz)
            if axis == 'x': got(at(here), cxr.at[p])
            else:
                here = wide
                got(at(here), czr.at[p, zz])
            chain(wide)
            give(here)

    mine = VO.at[:, x, y, z]
    own = [copy(wd.at[l], mine.at[l, :, c], own_s.at[l]) for l in range(L)]
    own += [copy(wgu.at[q, pl.ds(c, Z), c], mine.at[L + q, pl.ds(OWN * c, Z), c], own_s.at[L + q]) for q in range(HALF)]
    own += [copy(wgu.at[:, Z * oc, c], tmp.at[0], own_s.at[NP])]
    for cp in own: cp.start()
    b = pltpu.get_barrier_semaphore()
    def signal(to): pl.semaphore_signal(b, 1, device_id=to, device_id_type=MESH)
    for to in (NX, NY, NC, ZI): signal(to)
    @pl.when(mid)
    def _(): signal(ZO)
    pl.semaphore_wait(b, 4 + mid.astype(jnp.int32))
    swap = [remote(wgu.at[q, pl.ds(c, Z), oc], mine.at[L + q, pl.ds(OWN * c, Z), oc], ex_ss.at[q], ex_rs.at[q], NC) for q in range(HALF)]
    swap += [remote(wgu.at[:, Z * oc, oc], tmp.at[1], ex_ss.at[HALF], ex_rs.at[HALF], NC)]
    for cp in swap: cp.start()
    for cp in own[:L]: cp.wait()

    def round_(r):
        @pl.when(r == 1)
        def _():
            for cp in own[L:] + swap: cp.wait()
            upper = lax.broadcasted_iota(jnp.int32, T3, 1) % SUB < Z
            first = upper.astype(jnp.int32) == oc
            for q in range(HALF):
                VO[L + q, x, y, z, Z, c] = jnp.where(first, tmp[0, q].astype(F32), tmp[1, q].astype(F32)).astype(BF)
        for n, lag in order:
            p = r - lag
            @pl.when((p >= 0) & (p < NP))
            def _(): task(n, p)
    over(NP + max(lag for _, lag in order), round_)

    def finish(p):
        q = VO.at[pl.ds(0, 5), 0, 0, 0, :, 0]
        got(q, xs.at[p])
        got(q, ys.at[p])
        @pl.when(mid)
        def _():
            got(q.at[:, pl.ds(0, 6)], zis.at[p])
            got(q, zos.at[p])
        @pl.when(jnp.logical_not(mid))
        def _(): got(q.at[:, pl.ds(0, 3)], zis.at[p])
        whole = VO.at[0, :, :, :, :, 0]
        got(whole, ds.at[p])
        got(whole, dr.at[p])
    over(NP, finish)


def place_kernel(VO, og, ou, od, sems):
    out = []
    def put(src, dst):
        out.append(copy(src, dst, sems.at[len(out)]))
        out[-1].start()
    for l in range(L):
        for i in range(X):
            for k in range(CORES): put(VO.at[l, i, :, :, :, k], od.at[l, i, :, :, k])
            put(VO.at[L + l, i], og.at[l, i])
            put(VO.at[2 * L + l, i], ou.at[l, i])
    for cp in out: cp.wait()


def ag_call(wgu, wd):
    four = DMA((NP, Z))
    one = DMA((NP,))
    VO = pl.pallas_call(
        functools.partial(ag_kernel, lagged(AG_ORDER)),
        out_shape=VMEM((NP, X, Y, Z, U, CORES, *T3), BF),
        in_specs=[HB] * 2,
        out_specs=VM,
        scratch_shapes=[VMEM((2, HALF, *T3), BF), DMA((NP + 1,)), DMA((HALF + 1,)), DMA((HALF + 1,))] + [one] * 6 + [DMA((NP, Z, 2)), four, four, four, four, one, four, one, one],
        compiler_params=pltpu.CompilerParams(collective_id=1, has_side_effects=True, vmem_limit_bytes=2**20),
        name="all_gather",
    )(*(pltpu.with_memory_space_constraint(a, HBM) for a in (wgu, wd)))
    G = jax.ShapeDtypeStruct((L, X, Y, Z, U, CORES, *T3), BF)
    D = jax.ShapeDtypeStruct((L, X, Y, Z, CORES, U, *T3), BF)
    og, ou, od = pl.pallas_call(
        place_kernel, out_shape=(G, G, D), in_specs=[VM], out_specs=(ANY,) * 3, scratch_shapes=[DMA((16,))],
        compiler_params=pltpu.CompilerParams(vmem_limit_bytes=2**20), name="place",
    )(pltpu.with_memory_space_constraint(VO, VMEM))
    return og, ou, od


def solution(mesh):
    def step(*arrays):
        terms, weights, m, v = (arrays[i : i + 3] for i in range(0, 12, 3))
        Ggu, Gd, total, _ = rs_call(terms[0][0], terms[1][0], terms[2][0])
        Wgu, Wd, m, v = up_call(Ggu, Gd, total, weights, m, v)
        whole = [untiled(a, *w.shape[1:]) for a, w in zip(ag_call(Wgu, Wd), weights)]
        return (*whole, *m, *v)

    all_of, cut = P(None, None, None), P(None, "dp", None)
    return jax.shard_map(
        step,
        mesh=mesh,
        in_specs=(P(("rep", "dp"), None, None, None),) * 3 + (all_of,) * 3 + (cut,) * 6,
        out_specs=(P("rep", None, None),) * 3 + (P("rep", "dp", None),) * 6,
        check_vma=False,
    )
```

time: 1500 us -> 486 us (0.32)
  waiting for transfers between devices: 1170 us -> 0 us
  Pallas kernels: 0 us -> 485 us
  local copies, waits for them, and re-layouts: 248 us -> 0 us
  blocking collectives: 39.6 us -> 0 us
  other arithmetic: 24.8 us -> 0 us
  between operations: 16.9 us -> 0.67 us
    unnamed x8 -> x0, waiting for transfers between devices: 598 us -> none
    pallas_call x0 -> x4, Pallas kernels: none -> 485 us  [the longest x1 234 us: rs_call(): pl.pallas_call(functools.partial(rs_kernel, lagged(RS_ORDER)), out_shape=...]
    all_gather x3 -> x0, waiting for transfers between devices: 356 us -> none  [step(): whole = [lax.all_gather(one[0], 'dp', axis=1, tiled=True) for one in new]]
    unnamed x15 -> x0, local copies, waits for them, and re-layouts: 245 us -> none
    reduce_scatter x1 -> x0, waiting for transfers between devices: 219 us -> none  [step(): lax.psum_scatter(t[0], 'dp', scatter_dimension=1, tiled=True)]
    psum x1 -> x0, blocking collectives: 39.6 us -> none  [step(): squares = lax.psum(sum((jnp.sum(g * g) for g in gradients)), 'dp')]
    convert_element_type x3 -> x0, other arithmetic: 16.6 us -> none  [adamw(): return ((w - 0.02 * step).astype(jnp.bfloat16), m, v)]
  transfers between devices with their start and end apart: 6 -> 0, of which waited for: 6 -> 0; matrix products, arithmetic and copies ran while one was open for 10% -> 0% of each run, Pallas kernels for 0% -> 0%
where the time goes in v1:
time: 486 us
  Pallas kernels  485 us (100%)
    pallas_call x1, Pallas kernels, rs_call(): pl.pallas_call(functools.partial(rs_kernel, lagged(RS_ORDER)), out_shape=...  234 us
    pallas_call x1, Pallas kernels, ag_call(): pl.pallas_call(functools.partial(ag_kernel, lagged(AG_ORDER)), out_shape=...  222 us
    pallas_call x1, Pallas kernels, ag_call(): pl.pallas_call(place_kernel, out_shape=(G, G, D), in_specs=[VM], out_spec...  20.2 us

profile of v1, /device:TPU:0, one launch (start us, length us, event | category | flops | bytes accessed | tf_op | source)
XLA Modules:
  0.0 485.7 jit_solution(17796102444544885286)
XLA Ops:
  0.6 234.3 %reduce_scatter.1 = (bf16[2,2,5,2,9,16,128]{6,5,4,3,2,1,0:T(8,128)(2,1)S(1)}, bf16[2,9,9,16,128]{4,3,2,1,0:T(8,128)(2,1)S(1)}, f32[8,128]{1,0:T(8,128)S(1)}, bf16[6,2,2,4,9,9,16,128]{7,6,5,4,3,2,1,0:T(8,128)(2,1)}) custom-call(bf16[2,2,2,4,9,2,9,16,128]{8,7,6,5,4,3,2,1,0:T(8,128)(2,1)} %bitcast.92, bf16[2,2,2,4,9,2,9,16,128]{8,7,6,5,4,3,2,1,0:T(8,128)(2,1)} %bitcast.93, ...), custom_call_target="tpu_custom_call" | custom-call | tf_op jit(solution)/shard_map/reduce_scatter/pallas_call | solution.py:272
  234.9 8.1 %update.1 = (bf16[4,5,2,9,16,128]{5,4,3,2,1,0:T(8,128)(2,1)}, bf16[2,9,9,16,128]{4,3,2,1,0:T(8,128)(2,1)}, f32[36,36,2,128]{3,2,1,0:T(2,128)}, f32[36,36,2,128]{...) custom-call(bf16[2,2,5,2,9,16,128]{6,5,4,3,2,1,0:T(8,128)(2,1)S(1)} , ...), custom_call_target="tpu_custom_call" | custom-call | tf_op jit(solution)/shard_map/update/pallas_call | solution.py:354
  243.1 222.4 %all_gather.1.VO = bf16[6,2,2,4,9,2,9,16,128]{8,7,6,5,4,3,2,1,0:T(8,128)(2,1)S(1)} custom-call(bf16[4,5,2,9,16,128]{5,4,3,2,1,0:T(8,128)(2,1)} %get-tuple-element.26.wgu, bf16[2,9,9,16,128]{4,3,2,1,0:T(8,128)(2,1)} %get-tuple-element.27.wd), custom_call_target="tpu_custom_call" | custom-call | tf_op jit(solution)/shard_map/all_gather/pallas_call | solution.py:508
  465.5 20.2 %place.1 = (bf16[2,2,2,4,9,2,9,16,128]{8,7,6,5,4,3,2,1,0:T(8,128)(2,1)}, bf16[2,2,2,4,9,2,9,16,128]{8,7,6,5,4,3,2,1,0:T(8,128)(2,1)}, bf16[2,2,2,4,2,9,9,16,128]{8,7,6,5,4,3,2,1,0:T(8,128)(2,1)}) custom-call(bf16[6,2,2,4,9,2,9,16,128]{8,7,6,5,4,3,2,1,0:T(8,128)(2,1)S(1)} %all_gather.1.VO), custom_call_target="tpu_custom_call" | custom-call | tf_op jit(solution)/shard_map/place/pallas_call | solution.py:519

commit v2 on v1

--- a/solution.py
+++ b/solution.py
@@ -20,6 +20,9 @@
 HALF = NP - L
 OWN = 5
 PART = {'A': pl.ds(0, OWN), 'B': pl.ds(OWN, 3), 'C': U - 1}
+BLOCK, TILES = 36, 36
+RUN = TILES * L
+MOMENTS = (2, 2, BLOCK + 2 * Z, TILES, L, LANES)
 VM, HB, ANY = (pl.BlockSpec(memory_space=s) for s in (VMEM, HBM, pl.ANY))
 
 
@@ -61,6 +64,17 @@
 
 
 def got(ref, sem): copy(ref, ref, sem).wait()
+
+
+def greet(barrier, to, mid, too):
+    def signal(one): pl.semaphore_signal(barrier, 1, device_id=one, device_id_type=MESH)
+    for one in to: signal(one)
+    @pl.when(mid)
+    def _(): signal(too)
+    pl.semaphore_wait(barrier, len(to) + mid.astype(jnp.int32))
+
+
+def pinned(a, space): return pltpu.with_memory_space_constraint(a, space)
 
 
 def split(name): return name[0], name[1], int(name[-1]) if name[-1].isdigit() else 0
@@ -84,17 +98,17 @@
 LAST, CROSS = 2, 4
 
 
-def rs_kernel(order, gg, gu, gd, Ggu, Gd, TOT, PARTNER, *scr):
-    scr = iter(scr)
+def rs_kernel(order, gg, gu, gd, *refs):
+    moments, (Ggu, Gd, TOT, MOM, DOWN, PARTNER), scr = refs[:6], refs[6:12], iter(refs[12:])
     take = lambda names: {n: next(scr) for n in names}
     own, par, snd, rcv = take(CLASSES), take(CLASSES), take(CLASSES), take(ARRIVE)
-    fin, gx, acc, sall = take(range(4)).values()
+    fin, acc, sall = take(range(3)).values()
     own_s, par_s, snd_s, first_s, rcv_s = take(CLASSES), take(CLASSES), take(CLASSES), take(CLASSES), take(ARRIVE)
-    d2d_ss, d2d_rs, gx_ss, gx_rs, sa_ss, sa_rs = take(range(6)).values()
+    d2d_ss, d2d_rs, gx_ss, gx_rs, sa_ss, sa_rs, mom_s = take(range(7)).values()
     x, y, z, c = place()
     ox, oy, oc = 1 - x, 1 - y, 1 - c
     me = lax.axis_index("dp")
-    mid, near, inner, _ = line(z)
+    mid, near, inner, end = line(z)
     zo = near[::-1]
     side = z + 1 - 2 * (z % 2)
     NX, NY, NC = dev(ox, y, z, c), dev(x, oy, z, c), dev(x, y, z, oc)
@@ -214,15 +228,19 @@
             @pl.when(i != me)
             def _(): f((0, i))
         over(N, one)
-    others(lambda to: pl.semaphore_signal(b, 1, device_id=to, device_id_type=MESH))
-    pl.semaphore_wait(b, N - 1)
+    greet(b, (NX, NY, NC, dev(x, y, inner, c)), mid, dev(x, y, end, c))
     for n, _ in sorted(order, key=lambda t: t[1]): swap0(n).start()
     for p in range(1, NP):
         for cp in swap(p): cp.start()
 
     finlag = max(lag for n, lag in order if n[1] == 'f')
-    def rows(p): return remote(fin.at[p, pl.ds(Z * oc, OWN)], gx.at[p], gx_ss.at[p], gx_rs.at[p], NC)
+    def rows(p): return remote(fin.at[p, pl.ds(Z * oc, OWN)], Ggu.at[p // L, p % L, :, c], gx_ss.at[p], gx_rs.at[p], NC)
+    early = [copy(moments[k + 3 * i], MOM.at[k, i, pl.ds(Z, BLOCK)], mom_s.at[k, i]) for k in range(2) for i in range(2)]
+    early += [copy(moments[2 + 3 * i], DOWN.at[i], mom_s.at[2, i]) for i in range(2)]
     def round_(r):
+        @pl.when(r == 1)
+        def _():
+            for cp in early: cp.start()
         for i, (n, lag) in enumerate(order):
             p = r - lag
             @pl.when((p >= 0) & (p < NP))
@@ -246,11 +264,14 @@
     sall[me] = acc[0:SUB] + acc[SUB:ROWS]
     others(lambda to: remote(sall.at[me], sall.at[me], sa_ss, sa_rs, to).start())
     for l in range(L): Gd[l] = fin[HALF + l]
+    for k in range(2):
+        for i in range(2):
+            for at in (0, Z + BLOCK): MOM[k, i, at:at + Z] = jnp.zeros((Z, TILES, L, LANES), F32)
+    for cp in early: cp.wait()
     for p in range(HALF):
         k, l = p // L, p % L
         Ggu[k, l, :, c] = fin[p, pl.ds(Z * c, OWN)]
         rows(p).wait()
-        Ggu[k, l, :, oc] = gx[p]
     for n, lag in order:
         swap0(n).wait_send()
         if n[1] != 'f': send(n, NP - 1).wait_send()
@@ -262,47 +283,34 @@
     TOT[...] = jnp.sum(sall[...], axis=0)
 
 
-def rs_call(gg, gu, gd):
+def rs_call(gg, gu, gd, moments):
     bufs = [VMEM((len(names), *shape, *T3), BF) for shape, names in CLASSES.values()]
     sems = [DMA((len(names),)) for _, names in CLASSES.values()]
     scratch = bufs * 3 + [VMEM((NP, n, *CLASSES[cl][0], *T3), BF) for n, cl in ARRIVE.values()]
-    scratch += [VMEM((NP, U, *T3), BF), VMEM((HALF, OWN, *T3), BF), VMEM((ROWS, LANES), F32), VMEM((N, SUB, LANES), F32)]
+    scratch += [VMEM((NP, U, *T3), BF), VMEM((ROWS, LANES), F32), VMEM((N, SUB, LANES), F32)]
     scratch += sems * 4 + [DMA((NP, n)) for n, _ in ARRIVE.values()]
-    scratch += [DMA((NP, 4)), DMA((NP, 4)), DMA((HALF,)), DMA((HALF,)), DMA(()), DMA(())]
+    scratch += [DMA((NP, 4)), DMA((NP, 4)), DMA((HALF,)), DMA((HALF,)), DMA(()), DMA(()), DMA((3, 2))]
     return pl.pallas_call(
         functools.partial(rs_kernel, lagged(RS_ORDER)),
-        out_shape=(VMEM((2, L, OWN, CORES, *T3), BF), VMEM((L, U, *T3), BF), VMEM((SUB, LANES), F32), HBM((NP, X, Y, Z, U, *T3), BF)),
-        in_specs=[ANY] * 3,
-        out_specs=(VM, VM, VM, HB),
+        out_shape=(VMEM((2, L, OWN, CORES, *T3), BF), VMEM((L, U, *T3), BF), VMEM((SUB, LANES), F32), VMEM(MOMENTS, F32), VMEM((2, L, U, *T3), F32), HBM((NP, X, Y, Z, U, *T3), BF)),
+        in_specs=[HB] * 9,
+        out_specs=(VM, VM, VM, VM, VM, HB),
         scratch_shapes=scratch,
-        compiler_params=pltpu.CompilerParams(collective_id=0, has_side_effects=True, vmem_limit_bytes=58 * 2**20),
+        compiler_params=pltpu.CompilerParams(collective_id=0, has_side_effects=True, vmem_limit_bytes=53 * 2**20),
         name="reduce_scatter",
-    )(view_gu(gg), view_gu(gu), view_d(gd))
-
-
-BLOCK, TILES = 36, 36
-RUN = TILES * L
-
-
-def up_kernel(count, Ggu, Gd, TOT, wg, wu, wd, *refs):
-    moments, (Wgu, Wd), new, scr = refs[:6], refs[6:8], refs[8:14], refs[14:]
-    mom, dm, dv, wb, wdb, ld, st = scr
+    )(*(pinned(a, HBM) for a in (view_gu(gg), view_gu(gu), view_d(gd), *moments)))
+
+
+def up_kernel(count, Ggu, Gd, TOT, MOM, DOWN, wg, wu, wd, Wgu, Wd, *refs):
+    new, (mom, down, wb, wdb, ld, st, ds) = refs[:6], refs[6:]
     x, y, z, c = place()
-    loads, stores = [], []
-    def start(kept, sems, src, dst):
-        kept.append(copy(src, dst, sems.at[len(kept)]))
-        kept[-1].start()
-    load, store = functools.partial(start, loads, ld), functools.partial(start, stores, st)
-    rows = pl.ds(Z, BLOCK)
-    load(moments[2], dm)
-    load(moments[5], dv)
-    load(wd.at[:, x, y, z, c], wdb)
-    for k in range(2):
-        for i in range(2): load(moments[k + 3 * i], mom.at[k, i, rows])
-        load((wg, wu)[k].at[:, x, y, z, pl.ds(Z * c, OWN)], wb.at[k])
-    for k in range(2):
-        for i in range(2):
-            for at in (0, Z + BLOCK): mom[k, i, at:at + Z] = jnp.zeros((Z, TILES, L, LANES), F32)
+    loads = [copy(wd.at[:, x, y, z, c], wdb, ld.at[2])]
+    loads += [copy((wg, wu)[k].at[:, x, y, z, pl.ds(Z * c, OWN)], wb.at[k], ld.at[k]) for k in range(2)]
+    for cp in loads: cp.start()
+    stores = []
+    def store(src, dst):
+        stores.append(copy(src, dst, st.at[len(stores)]))
+        stores[-1].start()
     s = jnp.sum(jnp.sum(TOT[...], axis=0, keepdims=True), axis=1, keepdims=True)
     factor = jnp.minimum(1.0, 0.5 * lax.rsqrt(s * (1.0 / count) + 1e-30))
     def adamw(w, m, v, g):
@@ -310,21 +318,11 @@
         m = 0.9 * m + 0.1 * g
         v = 0.95 * v + 0.05 * g * g
         return w - 0.02 * (m * lax.rsqrt(v + 1e-8) + 0.1 * w), m, v
-    for cp in loads[:3]: cp.wait()
-    def down(l):
-        def unit(u):
-            for j in range(U):
-                at = (l, u, j)
-                w, dm[at], dv[at] = adamw(wdb[at].astype(F32), dm[at], dv[at], Gd[at].astype(F32))
-                wdb[at] = w.astype(BF)
-        over(U, unit)
-    over(L, down)
-    store(wdb, Wd)
-    store(dm, new[2])
-    store(dv, new[5])
+    rows = pl.ds(Z, BLOCK)
     for k in range(2):
-        for cp in loads[3 + 3 * k:][:3]: cp.wait()
-        M, V = (mom.at[k, i].reshape((BLOCK + 2 * Z) * RUN, LANES) for i in range(2))
+        loads[1 + k].wait()
+        flat = lambda ref, i: ref.at[k, i].reshape((BLOCK + 2 * Z) * RUN, LANES)
+        M, V, newM, newV = flat(MOM, 0), flat(MOM, 1), flat(mom, 0), flat(mom, 1)
         def tile(l, u, ch):
             base = (SUB * u + Z - Z * c) * RUN + TILES * ch + l
             for j in range(U):
@@ -333,13 +331,27 @@
                 for e in range(2):
                     at = pl.ds(base + (2 * j + e) * L, SUB, stride=RUN)
                     h = slice(SUB * e, SUB * e + SUB)
-                    wn, M[at, :], V[at, :] = adamw(w[h], M[at, :], V[at, :], g[h])
+                    wn, newM[at, :], newV[at, :] = adamw(w[h], M[at, :], V[at, :], g[h])
                     half.append(wn)
                 wb[k, l, u, ch, j] = jnp.concatenate(half).astype(BF)
         over(L, lambda l: over(OWN, lambda u: over(CORES, lambda ch: tile(l, u, ch))))
         store(wb.at[k], Wgu.at[pl.ds(L * k, L)])
         for i in range(2): store(mom.at[k, i, rows], new[k + 3 * i])
+    loads[0].wait()
+    def layer(l):
+        def unit(u):
+            for j in range(U):
+                at = (l, u, j)
+                w, m, v = adamw(wdb[at].astype(F32), DOWN[(0, *at)], DOWN[(1, *at)], Gd[at].astype(F32))
+                wdb[at] = w.astype(BF)
+                down[(0, *at)], down[(1, *at)] = m, v
+        over(U, unit)
+        for i in range(2): copy(down.at[i, l], new[2 + 3 * i].at[l], ds.at[i, l]).start()
+    over(L, layer)
+    store(wdb, Wd)
     for cp in stores: cp.wait()
+    for l in range(L):
+        for i in range(2): copy(down.at[i, l], new[2 + 3 * i].at[l], ds.at[i, l]).wait()
 
 
 def view_m(m): return m.reshape(L, BLOCK, TILES, LANES).transpose(1, 2, 0, 3)
@@ -347,25 +359,25 @@
 def view_md(m): return tiled(m).reshape(L, U, *T3)
 
 
-def up_call(Ggu, Gd, total, weights, m, v):
-    moments = [f(a) for a, f in zip((*m, *v), (view_m, view_m, view_md) * 2)]
+def up_call(Ggu, Gd, total, MOM, DOWN, weights, moments):
     count = sum(w.size for w in weights)
-    down = VMEM((L, U, *T3), F32)
+    W, Wd = (HALF, OWN, CORES, *T3), (L, U, *T3)
     res = pl.pallas_call(
         functools.partial(up_kernel, count),
-        out_shape=(HBM((HALF, OWN, CORES, *T3), BF), HBM((L, U, *T3), BF), *(HBM(a.shape, F32) for a in moments)),
-        in_specs=[VM] * 3 + [HB] * 9,
-        out_specs=(HB,) * 8,
-        scratch_shapes=[VMEM((2, 2, BLOCK + 2 * Z, TILES, L, LANES), F32), down, down, VMEM((2, L, OWN, CORES, *T3), BF), VMEM((L, U, *T3), BF), DMA((9,)), DMA((9,))],
+        out_shape=(HBM(W, BF), HBM(Wd, BF), *(HBM(a.shape, F32) for a in moments)),
+        in_specs=[VM] * 5 + [HB] * 3,
+        out_specs=[HB] * 8,
+        scratch_shapes=[VMEM(MOMENTS, F32), VMEM((2, *Wd), F32), VMEM((2, L, *W[1:]), BF), VMEM(Wd, BF), DMA((3,)), DMA((7,)), DMA((2, L))],
         compiler_params=pltpu.CompilerParams(vmem_limit_bytes=20 * 2**20),
         name="update",
     )(
-        *(pltpu.with_memory_space_constraint(a, VMEM) for a in (Ggu, Gd, total)),
-        *(pltpu.with_memory_space_constraint(a, HBM) for a in (view_gu(weights[0]), view_gu(weights[1]), view_d(weights[2]), *moments)),
+        *(pinned(a, VMEM) for a in (Ggu, Gd, total, MOM, DOWN)),
+        *(pinned(f(w), HBM) for f, w in zip((view_gu, view_gu, view_d), weights)),
     )
-    unview = (unview_m, unview_m, lambda a: untiled(a, *m[2].shape[1:]))
+    rows, columns = weights[2].shape[1:]
+    unview = (unview_m, unview_m, lambda a: untiled(a, rows // N, columns))
     new = [f(a) for a, f in zip(res[2:], unview * 2)]
-    return res[0], res[1], new[:3], new[3:]
+    return res[0], res[1], new
 
 
 AG_ORDER = ['Ax0_1+', 'Ax1_3++', 'By_0+', 'Cz_1+', 'Bo', 'Ay_2+', 'Co', 'Ao', 'Bz_2+', 'Ax0_2+', 'Ay_3+', 'Bx', 'Cy', 'By_1+', 'Cz_2+', 'Ax0_3+', 'Az_1', 'By_3+', 'Ax1_0+', 'Ay_0', 'Az_2', 'Cz_3+', 'Bz_1', 'Ax1_2+', 'Cx', 'Ay_1', 'Ax0_0+', 'By_2++', 'Az_3', 'Bz_3', 'Ax1_1+']
@@ -448,12 +460,7 @@
     own += [copy(wgu.at[q, pl.ds(c, Z), c], mine.at[L + q, pl.ds(OWN * c, Z), c], own_s.at[L + q]) for q in range(HALF)]
     own += [copy(wgu.at[:, Z * oc, c], tmp.at[0], own_s.at[NP])]
     for cp in own: cp.start()
-    b = pltpu.get_barrier_semaphore()
-    def signal(to): pl.semaphore_signal(b, 1, device_id=to, device_id_type=MESH)
-    for to in (NX, NY, NC, ZI): signal(to)
-    @pl.when(mid)
-    def _(): signal(ZO)
-    pl.semaphore_wait(b, 4 + mid.astype(jnp.int32))
+    greet(pltpu.get_barrier_semaphore(), (NX, NY, NC, ZI), mid, ZO)
     swap = [remote(wgu.at[q, pl.ds(c, Z), oc], mine.at[L + q, pl.ds(OWN * c, Z), oc], ex_ss.at[q], ex_rs.at[q], NC) for q in range(HALF)]
     swap += [remote(wgu.at[:, Z * oc, oc], tmp.at[1], ex_ss.at[HALF], ex_rs.at[HALF], NC)]
     for cp in swap: cp.start()
@@ -513,23 +520,24 @@
         scratch_shapes=[VMEM((2, HALF, *T3), BF), DMA((NP + 1,)), DMA((HALF + 1,)), DMA((HALF + 1,))] + [one] * 6 + [DMA((NP, Z, 2)), four, four, four, four, one, four, one, one],
         compiler_params=pltpu.CompilerParams(collective_id=1, has_side_effects=True, vmem_limit_bytes=2**20),
         name="all_gather",
-    )(*(pltpu.with_memory_space_constraint(a, HBM) for a in (wgu, wd)))
+    )(pinned(wgu, HBM), pinned(wd, HBM))
     G = jax.ShapeDtypeStruct((L, X, Y, Z, U, CORES, *T3), BF)
     D = jax.ShapeDtypeStruct((L, X, Y, Z, CORES, U, *T3), BF)
     og, ou, od = pl.pallas_call(
         place_kernel, out_shape=(G, G, D), in_specs=[VM], out_specs=(ANY,) * 3, scratch_shapes=[DMA((16,))],
         compiler_params=pltpu.CompilerParams(vmem_limit_bytes=2**20), name="place",
-    )(pltpu.with_memory_space_constraint(VO, VMEM))
+    )(pinned(VO, VMEM))
     return og, ou, od
 
 
 def solution(mesh):
     def step(*arrays):
         terms, weights, m, v = (arrays[i : i + 3] for i in range(0, 12, 3))
-        Ggu, Gd, total, _ = rs_call(terms[0][0], terms[1][0], terms[2][0])
-        Wgu, Wd, m, v = up_call(Ggu, Gd, total, weights, m, v)
+        moments = [f(a) for a, f in zip((*m, *v), (view_m, view_m, view_md) * 2)]
+        sums = rs_call(*(t[0] for t in terms), moments)
+        Wgu, Wd, new = up_call(*sums[:5], weights, moments)
         whole = [untiled(a, *w.shape[1:]) for a, w in zip(ag_call(Wgu, Wd), weights)]
-        return (*whole, *m, *v)
+        return (*whole, *new)
 
     all_of, cut = P(None, None, None), P(None, "dp", None)
     return jax.shard_map(

time: 486 us -> 485 us (level)
  no operation moved by 1% of the time
where the time goes in v2:
time: 485 us
  Pallas kernels  484 us (100%)
    pallas_call x1, Pallas kernels, rs_call(): pl.pallas_call(functools.partial(rs_kernel, lagged(RS_ORDER)), out_shape=...  234 us
    pallas_call x1, Pallas kernels, ag_call(): pl.pallas_call(functools.partial(ag_kernel, lagged(AG_ORDER)), out_shape=...  223 us
    pallas_call x1, Pallas kernels, ag_call(): pl.pallas_call(place_kernel, out_shape=(G, G, D), in_specs=[VM], out_spec...  20.2 us

profile of v2, /device:TPU:0, one launch (start us, length us, event | category | flops | bytes accessed | tf_op | source)
XLA Modules:
  0.0 484.9 jit_solution(3085101459573796337)
XLA Ops:
  0.6 233.5 %reduce_scatter.1 = (bf16[2,2,5,2,9,16,128]{6,5,4,3,2,1,0:T(8,128)(2,1)S(1)}, bf16[2,9,9,16,128]{4,3,2,1,0:T(8,128)(2,1)S(1)}, f32[8,128]{1,0:T(8,128)S(1)}, f32...) custom-call(bf16[2,2,2,4,9,2,9,16,128]{8,7,6,5,4,3,2,1,0:T(8,128)(2,, ...), custom_call_target="tpu_custom_call" | custom-call | tf_op jit(solution)/shard_map/reduce_scatter/pallas_call | solution.py:293
  234.2 7.5 %update.1 = (bf16[4,5,2,9,16,128]{5,4,3,2,1,0:T(8,128)(2,1)}, bf16[2,9,9,16,128]{4,3,2,1,0:T(8,128)(2,1)}, f32[36,36,2,128]{3,2,1,0:T(2,128)}, f32[36,36,2,128]{...) custom-call(bf16[2,2,5,2,9,16,128]{6,5,4,3,2,1,0:T(8,128)(2,1)S(1)} , ...), custom_call_target="tpu_custom_call" | custom-call | tf_op jit(solution)/shard_map/update/pallas_call | solution.py:365
  241.7 222.9 %all_gather.1.VO = bf16[6,2,2,4,9,2,9,16,128]{8,7,6,5,4,3,2,1,0:T(8,128)(2,1)S(1)} custom-call(bf16[4,5,2,9,16,128]{5,4,3,2,1,0:T(8,128)(2,1)} %get-tuple-element.30.wgu, bf16[2,9,9,16,128]{4,3,2,1,0:T(8,128)(2,1)} %get-tuple-element.31.wd), custom_call_target="tpu_custom_call" | custom-call | tf_op jit(solution)/shard_map/all_gather/pallas_call | solution.py:515
  464.6 20.2 %place.1 = (bf16[2,2,2,4,9,2,9,16,128]{8,7,6,5,4,3,2,1,0:T(8,128)(2,1)}, bf16[2,2,2,4,9,2,9,16,128]{8,7,6,5,4,3,2,1,0:T(8,128)(2,1)}, bf16[2,2,2,4,2,9,9,16,128]{8,7,6,5,4,3,2,1,0:T(8,128)(2,1)}) custom-call(bf16[6,2,2,4,9,2,9,16,128]{8,7,6,5,4,3,2,1,0:T(8,128)(2,1)S(1)} %all_gather.1.VO), custom_call_target="tpu_custom_call" | custom-call | tf_op jit(solution)/shard_map/place/pallas_call | solution.py:526

commit v3 on v2

--- a/solution.py
+++ b/solution.py
@@ -22,7 +22,7 @@
 PART = {'A': pl.ds(0, OWN), 'B': pl.ds(OWN, 3), 'C': U - 1}
 BLOCK, TILES = 36, 36
 RUN = TILES * L
-MOMENTS = (2, 2, BLOCK + 2 * Z, TILES, L, LANES)
+MOMENTS = (2, 2, OWN * SUB, TILES, L, LANES)
 VM, HB, ANY = (pl.BlockSpec(memory_space=s) for s in (VMEM, HBM, pl.ANY))
 
 
@@ -66,12 +66,13 @@
 def got(ref, sem): copy(ref, ref, sem).wait()
 
 
-def greet(barrier, to, mid, too):
+def greet(to, mid, too):
+    barrier = pltpu.get_barrier_semaphore()
     def signal(one): pl.semaphore_signal(barrier, 1, device_id=one, device_id_type=MESH)
     for one in to: signal(one)
     @pl.when(mid)
     def _(): signal(too)
-    pl.semaphore_wait(barrier, len(to) + mid.astype(jnp.int32))
+    return lambda: pl.semaphore_wait(barrier, len(to) + mid.astype(jnp.int32))
 
 
 def pinned(a, space): return pltpu.with_memory_space_constraint(a, space)
@@ -80,11 +81,14 @@
 def split(name): return name[0], name[1], int(name[-1]) if name[-1].isdigit() else 0
 
 
-def lagged(names): return [(n.rstrip('+'), n.count('+')) for n in names]
-
-
-RS_ORDER = ['By0', 'Ax0', 'Ax7+', 'Cz0', 'By2', 'Bf++', 'Az1+', 'Ax1', 'Ax4', 'Cz1', 'By1', 'Ax2', 'Cz2', 'Ax6', 'Ax5', 'Bx+', 'Ay0', 'Bz0', 'Ay1', 'Bz2', 'Ax3', 'By3', 'Bz1', 'Ay2', 'Az0', 'Cx', 'Ay3+', 'Az2+', 'Af++', 'Cf++', 'Cy+']
-TURN = 24
+def lagged(orders): return [[(n.rstrip('+'), n.count('+')) for n in names] for names in orders]
+
+
+RS_ORDER = [
+    ['Cz0', 'By0', 'Ax0', 'Cz2', 'Az0+', 'By1', 'Cz1', 'Ay1+', 'Ax4', 'Ax5', 'Ay3++', 'Az2++', 'By2', 'Bz0', 'Cy++', 'Ay2+', 'Az1+', 'Ax1', 'Ay0', 'Bx++', 'Ax2', 'By3+', 'Ax6+', 'Cx+', 'Ax7+', 'Af++', 'Bz1', 'Bz2+', 'Cf++', 'Ax3', 'Bf++'],
+    ['Cz1+', 'Cz2+', 'By1', 'Ax0', 'Ax1', 'Ay2+', 'Ax7++', 'Az1++', 'By0', 'Ax2', 'Ay0', 'Bz1+', 'Az2++', 'Cz0', 'Cy++', 'Ax4', 'Ax3', 'Bx++', 'By3+', 'Ax6+', 'By2', 'Bz2+', 'Az0+', 'Ax5', 'Ay1', 'Ay3+', 'Cx+', 'Bz0', 'Af++', 'Cf++', 'Bf++'],
+]
+AHEAD = 5
 CLASSES = {
     'A': ((OWN,), ['Ax0', 'Ax1', 'Ax2', 'Ax3', 'Ax4', 'Ax5', 'Ax6', 'Ax7', 'Ay0', 'Ay1', 'Ay2', 'Ay3', 'Az0', 'Az1', 'Az2', 'Af']),
     'By': ((X, 3), ['By0', 'By1', 'By2', 'By3', 'Bz0', 'Bz1', 'Bz2']),
@@ -98,8 +102,8 @@
 LAST, CROSS = 2, 4
 
 
-def rs_kernel(order, gg, gu, gd, *refs):
-    moments, (Ggu, Gd, TOT, MOM, DOWN, PARTNER), scr = refs[:6], refs[6:12], iter(refs[12:])
+def rs_kernel(orders, gg, gu, gd, wg, wu, *refs):
+    moments, (Ggu, Gd, TOT, MOM, DOWN, WGU, PARTNER), scr = refs[:6], refs[6:13], iter(refs[13:])
     take = lambda names: {n: next(scr) for n in names}
     own, par, snd, rcv = take(CLASSES), take(CLASSES), take(CLASSES), take(ARRIVE)
     fin, acc, sall = take(range(3)).values()
@@ -139,12 +143,12 @@
             @pl.when(p > 0)
             def _(): copy(PARTNER.at[(p, *b)], par[cl].at[i], par_s[cl].at[i]).start()
 
-    def send(name, p):
+    def send(name, p, middle):
         cl, i = CLASS_OF[name]
         n, axis, j = split(name)
         if axis == 'x': to, slot = NX, j
         elif axis == 'y': to, slot = NY, j
-        elif j < 2: to, slot = dev(x, y, inner, c), j + 3 * mid.astype(jnp.int32)
+        elif j < 2: to, slot = dev(x, y, inner, c), j + 3 * middle
         else: to, slot = dev(x, y, side, c), LAST
         kind = name[:2]
         return remote(snd[cl].at[i], rcv[kind].at[p, slot], snd_s[cl].at[i], rcv_s[kind].at[p, slot], to)
@@ -161,7 +165,7 @@
         elif len(lead) == 1: over(lead[0], one)
         else: over(lead[0], lambda i: over(lead[1], lambda j: one(i, j)))
 
-    def task(name, p):
+    def task(name, p, middle):
         cl, i = CLASS_OF[name]
         n, axis, j = split(name)
         lead = CLASSES[cl][0]
@@ -194,23 +198,15 @@
                 if name == 'Bf': refs += [R('Bx', 0)]
                 if name == 'Cy': refs += [R('Cx', 0).at[oy]]
                 if name == 'Cf': refs += [R('Cx', 0).at[y], R('Cy', 0)]
-        arrive(*wait)
+        arrive(*wait, *(farwait if middle else []))
         last = axis == 'f'
         if last: dst = fin.at[p, PART[n]]
         else:
             @pl.when(p > 0)
-            def _(): send(name, p).wait_send()
+            def _(): send(name, p, middle).wait_send()
             dst = snd[cl].at[i]
-        refs = [own[cl].at[i], par[cl].at[i]] + refs
-        if far:
-            @pl.when(mid)
-            def _():
-                arrive(*farwait)
-                add(dst, refs + far, lead, last)
-            @pl.when(jnp.logical_not(mid))
-            def _(): add(dst, refs, lead, last)
-        else: add(dst, refs, lead, last)
-        if not last: send(name, p).start()
+        add(dst, [own[cl].at[i], par[cl].at[i]] + refs + (far if middle else []), lead, last)
+        if not last: send(name, p, middle).start()
 
     def swap0(name):
         cl, i = CLASS_OF[name]
@@ -220,61 +216,72 @@
         parts = [(ox, ALL, ALL, PART['A']), (ALL, ALL, ALL, PART['B']), (ALL, ALL, ALL, PART['C']), (x, ALL, ALL, PART['A'])]
         return [remote(cut(p // L, p % L, q, oc), PARTNER.at[(p, *q)], d2d_ss.at[p, i], d2d_rs.at[p, i], NC) for i, q in enumerate(parts)]
 
+    met = greet((NX, NY, NC, dev(x, y, inner, c)), mid, dev(x, y, end, c))
     acc[...] = jnp.zeros_like(acc)
-    for n, _ in order: reload(n, jnp.int32(0))
-    b = pltpu.get_barrier_semaphore()
+    for n in CLASS_OF: reload(n, jnp.int32(0))
     def others(f):
         def one(i):
             @pl.when(i != me)
             def _(): f((0, i))
         over(N, one)
-    greet(b, (NX, NY, NC, dev(x, y, inner, c)), mid, dev(x, y, end, c))
-    for n, _ in sorted(order, key=lambda t: t[1]): swap0(n).start()
+    met()
+    def both(f):
+        for middle, order in enumerate(orders):
+            @pl.when(mid if middle else jnp.logical_not(mid))
+            def _(): f(order, middle)
+    def swaps0(order, middle):
+        for n, _ in sorted(order, key=lambda t: t[1]): swap0(n).start()
+    both(swaps0)
     for p in range(1, NP):
         for cp in swap(p): cp.start()
 
-    finlag = max(lag for n, lag in order if n[1] == 'f')
     def rows(p): return remote(fin.at[p, pl.ds(Z * oc, OWN)], Ggu.at[p // L, p % L, :, c], gx_ss.at[p], gx_rs.at[p], NC)
-    early = [copy(moments[k + 3 * i], MOM.at[k, i, pl.ds(Z, BLOCK)], mom_s.at[k, i]) for k in range(2) for i in range(2)]
+    early = [copy(moments[k + 3 * i], MOM.at[k, i, pl.ds(Z * c, BLOCK)], mom_s.at[k, i]) for k in range(2) for i in range(2)]
     early += [copy(moments[2 + 3 * i], DOWN.at[i], mom_s.at[2, i]) for i in range(2)]
-    def round_(r):
+    early += [copy((wg, wu)[k].at[:, x, y, z, pl.ds(Z * c, OWN)], WGU.at[k], mom_s.at[3, k]) for k in range(2)]
+    def part_of(name): return {'B': 1, 'C': 2}.get(name[0], 0 if name[1] == 'x' else 3)
+    def round_(r, order, middle):
+        heads = {}
+        for lag in range(3):
+            for n, own_lag in order:
+                if own_lag == lag: heads.setdefault(part_of(n), n)
+        for i, (n, lag) in enumerate(order):
+            m, ml = order[(i + AHEAD) % len(order)]
+            q = r + (i + AHEAD) // len(order) - ml
+            @pl.when((q > 0) & (q < NP))
+            def _():
+                if heads[part_of(m)] == m:
+                    for k in range(1, NP):
+                        @pl.when(q == k)
+                        def _(): swap(k)[part_of(m)].wait_recv()
+                reload(m, q)
+            p = r - lag
+            @pl.when((p >= 0) & (p < NP))
+            def _(): task(n, p, middle)
+        q = r - max(lag for n, lag in order if n[1] == 'f')
+        @pl.when((q >= 0) & (q < HALF))
+        def _(): rows(q).start()
+    def rounds(r):
         @pl.when(r == 1)
         def _():
             for cp in early: cp.start()
-        for i, (n, lag) in enumerate(order):
-            p = r - lag
-            @pl.when((p >= 0) & (p < NP))
-            def _(): task(n, p)
-            if i == TURN:
-                for q in range(1, NP):
-                    @pl.when(q == r + 1)
-                    def _():
-                        for cp in swap(q): cp.wait_recv()
-                for m, ml in order[:TURN]:
-                    @pl.when(r >= ml)
-                    def _(): reload(m, r - ml + 1)
-            if i >= TURN:
-                @pl.when(p >= 0)
-                def _(): reload(n, p + 1)
-        q = r - finlag
-        @pl.when((q >= 0) & (q < HALF))
-        def _(): rows(q).start()
-    over(NP + max(lag for _, lag in order), round_)
+        both(functools.partial(round_, r))
+    over(NP + max(lag for order in orders for _, lag in order), rounds)
 
     sall[me] = acc[0:SUB] + acc[SUB:ROWS]
     others(lambda to: remote(sall.at[me], sall.at[me], sa_ss, sa_rs, to).start())
     for l in range(L): Gd[l] = fin[HALF + l]
     for k in range(2):
         for i in range(2):
-            for at in (0, Z + BLOCK): MOM[k, i, at:at + Z] = jnp.zeros((Z, TILES, L, LANES), F32)
+            MOM[k, i, pl.ds(BLOCK * oc, Z)] = jnp.zeros((Z, TILES, L, LANES), F32)
     for cp in early: cp.wait()
     for p in range(HALF):
         k, l = p // L, p % L
         Ggu[k, l, :, c] = fin[p, pl.ds(Z * c, OWN)]
         rows(p).wait()
-    for n, lag in order:
+    for n in CLASS_OF:
         swap0(n).wait_send()
-        if n[1] != 'f': send(n, NP - 1).wait_send()
+        if n[1] != 'f': send(n, NP - 1, 0).wait_send()
     for p in range(1, NP):
         for cp in swap(p): cp.wait_send()
     rest = sall.at[pl.ds(0, N - 1)]
@@ -283,30 +290,30 @@
     TOT[...] = jnp.sum(sall[...], axis=0)
 
 
-def rs_call(gg, gu, gd, moments):
+def rs_call(terms, weights, moments):
     bufs = [VMEM((len(names), *shape, *T3), BF) for shape, names in CLASSES.values()]
     sems = [DMA((len(names),)) for _, names in CLASSES.values()]
     scratch = bufs * 3 + [VMEM((NP, n, *CLASSES[cl][0], *T3), BF) for n, cl in ARRIVE.values()]
     scratch += [VMEM((NP, U, *T3), BF), VMEM((ROWS, LANES), F32), VMEM((N, SUB, LANES), F32)]
     scratch += sems * 4 + [DMA((NP, n)) for n, _ in ARRIVE.values()]
-    scratch += [DMA((NP, 4)), DMA((NP, 4)), DMA((HALF,)), DMA((HALF,)), DMA(()), DMA(()), DMA((3, 2))]
+    scratch += [DMA((NP, 4)), DMA((NP, 4)), DMA((HALF,)), DMA((HALF,)), DMA(()), DMA(()), DMA((4, 2))]
+    views = view_gu, view_gu, view_d
     return pl.pallas_call(
         functools.partial(rs_kernel, lagged(RS_ORDER)),
-        out_shape=(VMEM((2, L, OWN, CORES, *T3), BF), VMEM((L, U, *T3), BF), VMEM((SUB, LANES), F32), VMEM(MOMENTS, F32), VMEM((2, L, U, *T3), F32), HBM((NP, X, Y, Z, U, *T3), BF)),
-        in_specs=[HB] * 9,
-        out_specs=(VM, VM, VM, VM, VM, HB),
+        out_shape=(VMEM((2, L, OWN, CORES, *T3), BF), VMEM((L, U, *T3), BF), VMEM((SUB, LANES), F32), VMEM(MOMENTS, F32), VMEM((2, L, U, *T3), F32), VMEM((2, L, OWN, CORES, *T3), BF), HBM((NP, X, Y, Z, U, *T3), BF)),
+        in_specs=[HB] * 11,
+        out_specs=(VM,) * 6 + (HB,),
         scratch_shapes=scratch,
-        compiler_params=pltpu.CompilerParams(collective_id=0, has_side_effects=True, vmem_limit_bytes=53 * 2**20),
+        compiler_params=pltpu.CompilerParams(collective_id=0, has_side_effects=True, vmem_limit_bytes=54_800_000),
         name="reduce_scatter",
-    )(*(pinned(a, HBM) for a in (view_gu(gg), view_gu(gu), view_d(gd), *moments)))
-
-
-def up_kernel(count, Ggu, Gd, TOT, MOM, DOWN, wg, wu, wd, Wgu, Wd, *refs):
+    )(*(pinned(a, HBM) for a in (*(f(a) for f, a in zip(views * 2, (*terms, *weights[:2]))), *moments)))
+
+
+def up_kernel(count, Ggu, Gd, TOT, MOM, DOWN, WGU, wd, Wgu, Wd, *refs):
     new, (mom, down, wb, wdb, ld, st, ds) = refs[:6], refs[6:]
     x, y, z, c = place()
-    loads = [copy(wd.at[:, x, y, z, c], wdb, ld.at[2])]
-    loads += [copy((wg, wu)[k].at[:, x, y, z, pl.ds(Z * c, OWN)], wb.at[k], ld.at[k]) for k in range(2)]
-    for cp in loads: cp.start()
+    load = copy(wd.at[:, x, y, z, c], wdb, ld)
+    load.start()
     stores = []
     def store(src, dst):
         stores.append(copy(src, dst, st.at[len(stores)]))
@@ -318,15 +325,14 @@
         m = 0.9 * m + 0.1 * g
         v = 0.95 * v + 0.05 * g * g
         return w - 0.02 * (m * lax.rsqrt(v + 1e-8) + 0.1 * w), m, v
-    rows = pl.ds(Z, BLOCK)
+    rows = pl.ds(Z * c, BLOCK)
     for k in range(2):
-        loads[1 + k].wait()
-        flat = lambda ref, i: ref.at[k, i].reshape((BLOCK + 2 * Z) * RUN, LANES)
+        flat = lambda ref, i: ref.at[k, i].reshape(OWN * SUB * RUN, LANES)
         M, V, newM, newV = flat(MOM, 0), flat(MOM, 1), flat(mom, 0), flat(mom, 1)
         def tile(l, u, ch):
-            base = (SUB * u + Z - Z * c) * RUN + TILES * ch + l
+            base = SUB * u * RUN + TILES * ch + l
             for j in range(U):
-                g, w = Ggu[k, l, u, ch, j].astype(F32), wb[k, l, u, ch, j].astype(F32)
+                g, w = Ggu[k, l, u, ch, j].astype(F32), WGU[k, l, u, ch, j].astype(F32)
                 half = []
                 for e in range(2):
                     at = pl.ds(base + (2 * j + e) * L, SUB, stride=RUN)
@@ -337,7 +343,7 @@
         over(L, lambda l: over(OWN, lambda u: over(CORES, lambda ch: tile(l, u, ch))))
         store(wb.at[k], Wgu.at[pl.ds(L * k, L)])
         for i in range(2): store(mom.at[k, i, rows], new[k + 3 * i])
-    loads[0].wait()
+    load.wait()
     def layer(l):
         def unit(u):
             for j in range(U):
@@ -359,38 +365,38 @@
 def view_md(m): return tiled(m).reshape(L, U, *T3)
 
 
-def up_call(Ggu, Gd, total, MOM, DOWN, weights, moments):
+def up_call(sums, weights, moments):
     count = sum(w.size for w in weights)
     W, Wd = (HALF, OWN, CORES, *T3), (L, U, *T3)
     res = pl.pallas_call(
         functools.partial(up_kernel, count),
         out_shape=(HBM(W, BF), HBM(Wd, BF), *(HBM(a.shape, F32) for a in moments)),
-        in_specs=[VM] * 5 + [HB] * 3,
+        in_specs=[VM] * 6 + [HB],
         out_specs=[HB] * 8,
-        scratch_shapes=[VMEM(MOMENTS, F32), VMEM((2, *Wd), F32), VMEM((2, L, *W[1:]), BF), VMEM(Wd, BF), DMA((3,)), DMA((7,)), DMA((2, L))],
+        scratch_shapes=[VMEM(MOMENTS, F32), VMEM((2, *Wd), F32), VMEM((2, L, *W[1:]), BF), VMEM(Wd, BF), DMA(()), DMA((7,)), DMA((2, L))],
         compiler_params=pltpu.CompilerParams(vmem_limit_bytes=20 * 2**20),
         name="update",
-    )(
-        *(pinned(a, VMEM) for a in (Ggu, Gd, total, MOM, DOWN)),
-        *(pinned(f(w), HBM) for f, w in zip((view_gu, view_gu, view_d), weights)),
-    )
+    )(*(pinned(a, VMEM) for a in sums), pinned(view_d(weights[2]), HBM))
     rows, columns = weights[2].shape[1:]
     unview = (unview_m, unview_m, lambda a: untiled(a, rows // N, columns))
     new = [f(a) for a, f in zip(res[2:], unview * 2)]
     return res[0], res[1], new
 
 
-AG_ORDER = ['Ax0_1+', 'Ax1_3++', 'By_0+', 'Cz_1+', 'Bo', 'Ay_2+', 'Co', 'Ao', 'Bz_2+', 'Ax0_2+', 'Ay_3+', 'Bx', 'Cy', 'By_1+', 'Cz_2+', 'Ax0_3+', 'Az_1', 'By_3+', 'Ax1_0+', 'Ay_0', 'Az_2', 'Cz_3+', 'Bz_1', 'Ax1_2+', 'Cx', 'Ay_1', 'Ax0_0+', 'By_2++', 'Az_3', 'Bz_3', 'Ax1_1+']
-
-
-def ag_kernel(order, wgu, wd, VO, tmp, own_s, ex_ss, ex_rs, xs, ys, zis, zos, ds, dr, axr, ayr, azr, byr, bzr, bxr, czr, cxr, cyr):
+AG_ORDER = [
+    ['Bo', 'Co', 'Ax0_0++', 'Ao', 'Cx+', 'By_0++', 'Az_2+', 'Ay_1+', 'Ax0_3++', 'Bz_3++', 'By_1++', 'Bz_1+', 'Cy', 'Ax1_1++', 'Ay_3++', 'Cz_2++', 'Ax0_2++', 'Cz_1++', 'Az_3+', 'Bx', 'By_2++', 'Bz_2+', 'Ay_2+', 'Ax1_2++', 'Ax1_0+', 'Ax0_1+', 'Ay_0', 'Ax1_3++', 'Az_1', 'Cz_3++', 'By_3++'],
+    ['Co', 'Bo+', 'Bz_3++', 'Ao', 'Az_2+', 'Az_1+', 'Ay_2++', 'Cx++', 'Ax0_0+', 'Cz_2++', 'Bx+', 'Ay_3++', 'Ax0_3++', 'Az_3+', 'Cz_3++', 'By_2++', 'Cy+', 'Bz_1+', 'Ax1_1++', 'Ay_1+', 'By_0++', 'Bz_2+', 'Ay_0+', 'Ax0_2++', 'By_1++', 'Ax1_0++', 'Ax0_1++', 'Ax1_2++', 'Ax1_3++', 'Cz_1+', 'By_3++'],
+]
+
+
+def ag_kernel(orders, wgu, wd, VO, tmp, own_s, ex_ss, ex_rs, xs, ys, zis, zos, ds, dr, axr, ayr, azr, byr, bzr, bxr, czr, cxr, cyr):
     x, y, z, c = place()
     ox, oy, oc = 1 - x, 1 - y, 1 - c
     mid, sl, inner, end = line(z)
     NX, NY, NC, ZI, ZO = dev(ox, y, z, c), dev(x, oy, z, c), dev(x, y, z, oc), dev(x, y, inner, c), dev(x, y, end, c)
     zr = {'A': azr, 'B': bzr, 'C': czr}
 
-    def task(name, p):
+    def task(name, p, middle):
         n, axis, i = split(name)
         zz = sl[i]
         def at(idx): return VO.at[(p, *idx, PART[n], c)]
@@ -398,11 +404,8 @@
         def give(idx): push(idx, NC, ds, dr.at[p])
         def chain(idx):
             rs = zr[n].at[p, zz]
-            if i == 0: push(idx, ZI, zis, rs)
-            @pl.when(mid)
-            def _():
-                if i == 1: push(idx, ZI, zis, rs)
-                else: push(idx, ZO, zos, rs)
+            if i == 0 or middle and i == 1: push(idx, ZI, zis, rs)
+            if middle and i != 1: push(idx, ZO, zos, rs)
         if axis == 'o':
             here = x, y, z
             if n == 'A':
@@ -455,12 +458,13 @@
             chain(wide)
             give(here)
 
+    met = greet((NX, NY, NC, ZI), mid, ZO)
     mine = VO.at[:, x, y, z]
     own = [copy(wd.at[l], mine.at[l, :, c], own_s.at[l]) for l in range(L)]
     own += [copy(wgu.at[q, pl.ds(c, Z), c], mine.at[L + q, pl.ds(OWN * c, Z), c], own_s.at[L + q]) for q in range(HALF)]
     own += [copy(wgu.at[:, Z * oc, c], tmp.at[0], own_s.at[NP])]
     for cp in own: cp.start()
-    greet(pltpu.get_barrier_semaphore(), (NX, NY, NC, ZI), mid, ZO)
+    met()
     swap = [remote(wgu.at[q, pl.ds(c, Z), oc], mine.at[L + q, pl.ds(OWN * c, Z), oc], ex_ss.at[q], ex_rs.at[q], NC) for q in range(HALF)]
     swap += [remote(wgu.at[:, Z * oc, oc], tmp.at[1], ex_ss.at[HALF], ex_rs.at[HALF], NC)]
     for cp in swap: cp.start()
@@ -474,11 +478,14 @@
             first = upper.astype(jnp.int32) == oc
             for q in range(HALF):
                 VO[L + q, x, y, z, Z, c] = jnp.where(first, tmp[0, q].astype(F32), tmp[1, q].astype(F32)).astype(BF)
-        for n, lag in order:
-            p = r - lag
-            @pl.when((p >= 0) & (p < NP))
-            def _(): task(n, p)
-    over(NP + max(lag for _, lag in order), round_)
+        for middle, order in enumerate(orders):
+            @pl.when(mid if middle else jnp.logical_not(mid))
+            def _():
+                for n, lag in order:
+                    p = r - lag
+                    @pl.when((p >= 0) & (p < NP))
+                    def _(): task(n, p, middle)
+    over(NP + max(lag for order in orders for _, lag in order), round_)
 
     def finish(p):
         q = VO.at[pl.ds(0, 5), 0, 0, 0, :, 0]
@@ -534,8 +541,8 @@
     def step(*arrays):
         terms, weights, m, v = (arrays[i : i + 3] for i in range(0, 12, 3))
         moments = [f(a) for a, f in zip((*m, *v), (view_m, view_m, view_md) * 2)]
-        sums = rs_call(*(t[0] for t in terms), moments)
-        Wgu, Wd, new = up_call(*sums[:5], weights, moments)
+        *sums, _ = rs_call([t[0] for t in terms], weights, moments)
+        Wgu, Wd, new = up_call(sums, weights, moments)
         whole = [untiled(a, *w.shape[1:]) for a, w in zip(ag_call(Wgu, Wd), weights)]
         return (*whole, *new)
 

time: 485 us -> 479 us (0.988)
  Pallas kernels: 484 us -> 478 us
where the time goes in v3:
time: 479 us
  Pallas kernels  478 us (100%)
    pallas_call x1, Pallas kernels, rs_call(): pl.pallas_call(functools.partial(rs_kernel, lagged(RS_ORDER)), out_shape=...  230 us
    pallas_call x1, Pallas kernels, ag_call(): pl.pallas_call(functools.partial(ag_kernel, lagged(AG_ORDER)), out_shape=...  221 us
    pallas_call x1, Pallas kernels, ag_call(): pl.pallas_call(place_kernel, out_shape=(G, G, D), in_specs=[VM], out_spec...  20.2 us

profile of v3, /device:TPU:0, one launch (start us, length us, event | category | flops | bytes accessed | tf_op | source)
XLA Modules:
  0.0 478.8 jit_solution(513613821182269975)
XLA Ops:
  0.6 230.4 %reduce_scatter.1 = (bf16[2,2,5,2,9,16,128]{6,5,4,3,2,1,0:T(8,128)(2,1)S(1)}, bf16[2,9,9,16,128]{4,3,2,1,0:T(8,128)(2,1)S(1)}, f32[8,128]{1,0:T(8,128)S(1)}, f32...) custom-call(bf16[2,2,2,4,9,2,9,16,128]{8,7,6,5,4,3,2,1,0:T(8,128)(2,, ...), custom_call_target="tpu_custom_call" | custom-call | tf_op jit(solution)/shard_map/reduce_scatter/pallas_call | solution.py:301
  231.1 6.2 %update.1 = (bf16[4,5,2,9,16,128]{5,4,3,2,1,0:T(8,128)(2,1)}, bf16[2,9,9,16,128]{4,3,2,1,0:T(8,128)(2,1)}, f32[36,36,2,128]{3,2,1,0:T(2,128)}, f32[36,36,2,128]{...) custom-call(bf16[2,2,5,2,9,16,128]{6,5,4,3,2,1,0:T(8,128)(2,1)S(1)} , ...), custom_call_target="tpu_custom_call" | custom-call | tf_op jit(solution)/shard_map/update/pallas_call | solution.py:371
  237.3 221.2 %all_gather.1.VO = bf16[6,2,2,4,9,2,9,16,128]{8,7,6,5,4,3,2,1,0:T(8,128)(2,1)S(1)} custom-call(bf16[4,5,2,9,16,128]{5,4,3,2,1,0:T(8,128)(2,1)} %get-tuple-element.32.wgu, bf16[2,9,9,16,128]{4,3,2,1,0:T(8,128)(2,1)} %get-tuple-element.33.wd), custom_call_target="tpu_custom_call" | custom-call | tf_op jit(solution)/shard_map/all_gather/pallas_call | solution.py:522
  458.6 20.2 %place.1 = (bf16[2,2,2,4,9,2,9,16,128]{8,7,6,5,4,3,2,1,0:T(8,128)(2,1)}, bf16[2,2,2,4,9,2,9,16,128]{8,7,6,5,4,3,2,1,0:T(8,128)(2,1)}, bf16[2,2,2,4,2,9,9,16,128]{8,7,6,5,4,3,2,1,0:T(8,128)(2,1)}) custom-call(bf16[6,2,2,4,9,2,9,16,128]{8,7,6,5,4,3,2,1,0:T(8,128)(2,1)S(1)} %all_gather.1.VO), custom_call_target="tpu_custom_call" | custom-call | tf_op jit(solution)/shard_map/place/pallas_call | solution.py:533

commit v4 on v3

--- a/solution.py
+++ b/solution.py
@@ -325,7 +325,6 @@
         m = 0.9 * m + 0.1 * g
         v = 0.95 * v + 0.05 * g * g
         return w - 0.02 * (m * lax.rsqrt(v + 1e-8) + 0.1 * w), m, v
-    rows = pl.ds(Z * c, BLOCK)
     for k in range(2):
         flat = lambda ref, i: ref.at[k, i].reshape(OWN * SUB * RUN, LANES)
         M, V, newM, newV = flat(MOM, 0), flat(MOM, 1), flat(mom, 0), flat(mom, 1)
@@ -340,9 +339,12 @@
                     wn, newM[at, :], newV[at, :] = adamw(w[h], M[at, :], V[at, :], g[h])
                     half.append(wn)
                 wb[k, l, u, ch, j] = jnp.concatenate(half).astype(BF)
-        over(L, lambda l: over(OWN, lambda u: over(CORES, lambda ch: tile(l, u, ch))))
+        for tiles, (row, n) in zip((range(3), range(3, OWN)), ((0, ROWS), (ROWS, BLOCK - ROWS))):
+            def both(u):
+                over(L, lambda l: [tile(l, tiles[0] + u, ch) for ch in range(CORES)])
+            over(len(tiles), both)
+            for i in range(2): store(mom.at[k, i, pl.ds(Z * c + row, n)], new[k + 3 * i].at[pl.ds(row, n)])
         store(wb.at[k], Wgu.at[pl.ds(L * k, L)])
-        for i in range(2): store(mom.at[k, i, rows], new[k + 3 * i])
     load.wait()
     def layer(l):
         def unit(u):
@@ -373,7 +375,7 @@
         out_shape=(HBM(W, BF), HBM(Wd, BF), *(HBM(a.shape, F32) for a in moments)),
         in_specs=[VM] * 6 + [HB],
         out_specs=[HB] * 8,
-        scratch_shapes=[VMEM(MOMENTS, F32), VMEM((2, *Wd), F32), VMEM((2, L, *W[1:]), BF), VMEM(Wd, BF), DMA(()), DMA((7,)), DMA((2, L))],
+        scratch_shapes=[VMEM(MOMENTS, F32), VMEM((2, *Wd), F32), VMEM((2, L, *W[1:]), BF), VMEM(Wd, BF), DMA(()), DMA((11,)), DMA((2, L))],
         compiler_params=pltpu.CompilerParams(vmem_limit_bytes=20 * 2**20),
         name="update",
     )(*(pinned(a, VMEM) for a in sums), pinned(view_d(weights[2]), HBM))

time: 479 us -> 479 us (level)
  no operation moved by 1% of the time
where the time goes in v4:
time: 479 us; the launch traced here: 478 us
  Pallas kernels  477 us (100%)
    pallas_call x1, Pallas kernels, rs_call(): pl.pallas_call(functools.partial(rs_kernel, lagged(RS_ORDER)), out_shape=...  230 us
    pallas_call x1, Pallas kernels, ag_call(): pl.pallas_call(functools.partial(ag_kernel, lagged(AG_ORDER)), out_shape=...  221 us
    pallas_call x1, Pallas kernels, ag_call(): pl.pallas_call(place_kernel, out_shape=(G, G, D), in_specs=[VM], out_spec...  20.2 us

profile of v4, /device:TPU:0, one launch (start us, length us, event | category | flops | bytes accessed | tf_op | source)
XLA Modules:
  0.0 478.1 jit_solution(10566341167331805880)
XLA Ops:
  0.6 230.4 %reduce_scatter.1 = (bf16[2,2,5,2,9,16,128]{6,5,4,3,2,1,0:T(8,128)(2,1)S(1)}, bf16[2,9,9,16,128]{4,3,2,1,0:T(8,128)(2,1)S(1)}, f32[8,128]{1,0:T(8,128)S(1)}, f32...) custom-call(bf16[2,2,2,4,9,2,9,16,128]{8,7,6,5,4,3,2,1,0:T(8,128)(2,, ...), custom_call_target="tpu_custom_call" | custom-call | tf_op jit(solution)/shard_map/reduce_scatter/pallas_call | solution.py:301
  231.1 5.5 %update.1 = (bf16[4,5,2,9,16,128]{5,4,3,2,1,0:T(8,128)(2,1)}, bf16[2,9,9,16,128]{4,3,2,1,0:T(8,128)(2,1)}, f32[36,36,2,128]{3,2,1,0:T(2,128)}, f32[36,36,2,128]{...) custom-call(bf16[2,2,5,2,9,16,128]{6,5,4,3,2,1,0:T(8,128)(2,1)S(1)} , ...), custom_call_target="tpu_custom_call" | custom-call | tf_op jit(solution)/shard_map/update/pallas_call | solution.py:373
  236.6 221.2 %all_gather.1.VO = bf16[6,2,2,4,9,2,9,16,128]{8,7,6,5,4,3,2,1,0:T(8,128)(2,1)S(1)} custom-call(bf16[4,5,2,9,16,128]{5,4,3,2,1,0:T(8,128)(2,1)} %get-tuple-element.32.wgu, bf16[2,9,9,16,128]{4,3,2,1,0:T(8,128)(2,1)} %get-tuple-element.33.wd), custom_call_target="tpu_custom_call" | custom-call | tf_op jit(solution)/shard_map/all_gather/pallas_call | solution.py:524
  457.8 20.2 %place.1 = (bf16[2,2,2,4,9,2,9,16,128]{8,7,6,5,4,3,2,1,0:T(8,128)(2,1)}, bf16[2,2,2,4,9,2,9,16,128]{8,7,6,5,4,3,2,1,0:T(8,128)(2,1)}, bf16[2,2,2,4,2,9,9,16,128]{8,7,6,5,4,3,2,1,0:T(8,128)(2,1)}) custom-call(bf16[6,2,2,4,9,2,9,16,128]{8,7,6,5,4,3,2,1,0:T(8,128)(2,1)S(1)} %all_gather.1.VO), custom_call_target="tpu_custom_call" | custom-call | tf_op jit(solution)/shard_map/place/pallas_call | solution.py:535

commit v5 on v4

--- a/solution.py
+++ b/solution.py
@@ -325,6 +325,19 @@
         m = 0.9 * m + 0.1 * g
         v = 0.95 * v + 0.05 * g * g
         return w - 0.02 * (m * lax.rsqrt(v + 1e-8) + 0.1 * w), m, v
+    def do_down():
+        load.wait()
+        def layer(l):
+            def unit(u):
+                for j in range(U):
+                    at = (l, u, j)
+                    w, m, v = adamw(wdb[at].astype(F32), DOWN[(0, *at)], DOWN[(1, *at)], Gd[at].astype(F32))
+                    wdb[at] = w.astype(BF)
+                    down[(0, *at)], down[(1, *at)] = m, v
+            over(U, unit)
+            for i in range(2): copy(down.at[i, l], new[2 + 3 * i].at[l], ds.at[i, l]).start()
+        over(L, layer)
+        store(wdb, Wd)
     for k in range(2):
         flat = lambda ref, i: ref.at[k, i].reshape(OWN * SUB * RUN, LANES)
         M, V, newM, newV = flat(MOM, 0), flat(MOM, 1), flat(mom, 0), flat(mom, 1)
@@ -339,24 +352,13 @@
                     wn, newM[at, :], newV[at, :] = adamw(w[h], M[at, :], V[at, :], g[h])
                     half.append(wn)
                 wb[k, l, u, ch, j] = jnp.concatenate(half).astype(BF)
-        for tiles, (row, n) in zip((range(3), range(3, OWN)), ((0, ROWS), (ROWS, BLOCK - ROWS))):
-            def both(u):
-                over(L, lambda l: [tile(l, tiles[0] + u, ch) for ch in range(CORES)])
-            over(len(tiles), both)
+        for u in range(OWN):
+            over(L, lambda l: [tile(l, u, ch) for ch in range(CORES)])
+            row = max(SUB * u - Z, 0)
+            n = Z if u == 0 else SUB
             for i in range(2): store(mom.at[k, i, pl.ds(Z * c + row, n)], new[k + 3 * i].at[pl.ds(row, n)])
-        store(wb.at[k], Wgu.at[pl.ds(L * k, L)])
-    load.wait()
-    def layer(l):
-        def unit(u):
-            for j in range(U):
-                at = (l, u, j)
-                w, m, v = adamw(wdb[at].astype(F32), DOWN[(0, *at)], DOWN[(1, *at)], Gd[at].astype(F32))
-                wdb[at] = w.astype(BF)
-                down[(0, *at)], down[(1, *at)] = m, v
-        over(U, unit)
-        for i in range(2): copy(down.at[i, l], new[2 + 3 * i].at[l], ds.at[i, l]).start()
-    over(L, layer)
-    store(wdb, Wd)
+            store(wb.at[k, :, u], Wgu.at[pl.ds(L * k, L), u])
+        if k == 0: do_down()
     for cp in stores: cp.wait()
     for l in range(L):
         for i in range(2): copy(down.at[i, l], new[2 + 3 * i].at[l], ds.at[i, l]).wait()
@@ -375,7 +377,7 @@
         out_shape=(HBM(W, BF), HBM(Wd, BF), *(HBM(a.shape, F32) for a in moments)),
         in_specs=[VM] * 6 + [HB],
         out_specs=[HB] * 8,
-        scratch_shapes=[VMEM(MOMENTS, F32), VMEM((2, *Wd), F32), VMEM((2, L, *W[1:]), BF), VMEM(Wd, BF), DMA(()), DMA((11,)), DMA((2, L))],
+        scratch_shapes=[VMEM(MOMENTS, F32), VMEM((2, *Wd), F32), VMEM((2, L, *W[1:]), BF), VMEM(Wd, BF), DMA(()), DMA((6 * OWN + 1,)), DMA((2, L))],
         compiler_params=pltpu.CompilerParams(vmem_limit_bytes=20 * 2**20),
         name="update",
     )(*(pinned(a, VMEM) for a in sums), pinned(view_d(weights[2]), HBM))

time: 479 us -> 478 us (level)
  no operation moved by 1% of the time
where the time goes in v5:
time: 478 us
  Pallas kernels  477 us (100%)
    pallas_call x1, Pallas kernels, rs_call(): pl.pallas_call(functools.partial(rs_kernel, lagged(RS_ORDER)), out_shape=...  230 us
    pallas_call x1, Pallas kernels, ag_call(): pl.pallas_call(functools.partial(ag_kernel, lagged(AG_ORDER)), out_shape=...  221 us
    pallas_call x1, Pallas kernels, ag_call(): pl.pallas_call(place_kernel, out_shape=(G, G, D), in_specs=[VM], out_spec...  20.2 us

profile of v5, /device:TPU:0, one launch (start us, length us, event | category | flops | bytes accessed | tf_op | source)
XLA Modules:
  0.0 477.7 jit_solution(5185852785855414050)
XLA Ops:
  0.6 230.4 %reduce_scatter.1 = (bf16[2,2,5,2,9,16,128]{6,5,4,3,2,1,0:T(8,128)(2,1)S(1)}, bf16[2,9,9,16,128]{4,3,2,1,0:T(8,128)(2,1)S(1)}, f32[8,128]{1,0:T(8,128)S(1)}, f32...) custom-call(bf16[2,2,2,4,9,2,9,16,128]{8,7,6,5,4,3,2,1,0:T(8,128)(2,, ...), custom_call_target="tpu_custom_call" | custom-call | tf_op jit(solution)/shard_map/reduce_scatter/pallas_call | solution.py:301
  231.1 5.1 %update.1 = (bf16[4,5,2,9,16,128]{5,4,3,2,1,0:T(8,128)(2,1)}, bf16[2,9,9,16,128]{4,3,2,1,0:T(8,128)(2,1)}, f32[36,36,2,128]{3,2,1,0:T(2,128)}, f32[36,36,2,128]{...) custom-call(bf16[2,2,5,2,9,16,128]{6,5,4,3,2,1,0:T(8,128)(2,1)S(1)} , ...), custom_call_target="tpu_custom_call" | custom-call | tf_op jit(solution)/shard_map/update/pallas_call | solution.py:375
  236.2 221.2 %all_gather.1.VO = bf16[6,2,2,4,9,2,9,16,128]{8,7,6,5,4,3,2,1,0:T(8,128)(2,1)S(1)} custom-call(bf16[4,5,2,9,16,128]{5,4,3,2,1,0:T(8,128)(2,1)} %get-tuple-element.32.wgu, bf16[2,9,9,16,128]{4,3,2,1,0:T(8,128)(2,1)} %get-tuple-element.33.wd), custom_call_target="tpu_custom_call" | custom-call | tf_op jit(solution)/shard_map/all_gather/pallas_call | solution.py:526
  457.5 20.2 %place.1 = (bf16[2,2,2,4,9,2,9,16,128]{8,7,6,5,4,3,2,1,0:T(8,128)(2,1)}, bf16[2,2,2,4,9,2,9,16,128]{8,7,6,5,4,3,2,1,0:T(8,128)(2,1)}, bf16[2,2,2,4,2,9,9,16,128]{8,7,6,5,4,3,2,1,0:T(8,128)(2,1)}) custom-call(bf16[6,2,2,4,9,2,9,16,128]{8,7,6,5,4,3,2,1,0:T(8,128)(2,1)S(1)} %all_gather.1.VO), custom_call_target="tpu_custom_call" | custom-call | tf_op jit(solution)/shard_map/place/pallas_call | solution.py:537

commit v6 on v5

--- a/solution.py
+++ b/solution.py
@@ -512,11 +512,12 @@
     def put(src, dst):
         out.append(copy(src, dst, sems.at[len(out)]))
         out[-1].start()
-    for l in range(L):
-        for i in range(X):
-            for k in range(CORES): put(VO.at[l, i, :, :, :, k], od.at[l, i, :, :, k])
-            put(VO.at[L + l, i], og.at[l, i])
-            put(VO.at[2 * L + l, i], ou.at[l, i])
+    parts = [(l, i) for l in range(L) for i in range(X)]
+    for l, i in parts:
+        put(VO.at[L + l, i], og.at[l, i])
+        put(VO.at[2 * L + l, i], ou.at[l, i])
+    for l, i in parts:
+        for k in range(CORES): put(VO.at[l, i, :, :, :, k], od.at[l, i, :, :, k])
     for cp in out: cp.wait()
 
 

time: 478 us -> 478 us (level)
  no operation moved by 1% of the time
where the time goes in v6:
time: 478 us
  Pallas kernels  477 us (100%)
    pallas_call x1, Pallas kernels, rs_call(): pl.pallas_call(functools.partial(rs_kernel, lagged(RS_ORDER)), out_shape=...  230 us
    pallas_call x1, Pallas kernels, ag_call(): pl.pallas_call(functools.partial(ag_kernel, lagged(AG_ORDER)), out_shape=...  221 us
    pallas_call x1, Pallas kernels, ag_call(): pl.pallas_call(place_kernel, out_shape=(G, G, D), in_specs=[VM], out_spec...  20.2 us

profile of v6, /device:TPU:0, one launch (start us, length us, event | category | flops | bytes accessed | tf_op | source)
XLA Modules:
  0.0 477.6 jit_solution(7408874909659753402)
XLA Ops:
  0.6 230.4 %reduce_scatter.1 = (bf16[2,2,5,2,9,16,128]{6,5,4,3,2,1,0:T(8,128)(2,1)S(1)}, bf16[2,9,9,16,128]{4,3,2,1,0:T(8,128)(2,1)S(1)}, f32[8,128]{1,0:T(8,128)S(1)}, f32...) custom-call(bf16[2,2,2,4,9,2,9,16,128]{8,7,6,5,4,3,2,1,0:T(8,128)(2,, ...), custom_call_target="tpu_custom_call" | custom-call | tf_op jit(solution)/shard_map/reduce_scatter/pallas_call | solution.py:301
  231.1 5.1 %update.1 = (bf16[4,5,2,9,16,128]{5,4,3,2,1,0:T(8,128)(2,1)}, bf16[2,9,9,16,128]{4,3,2,1,0:T(8,128)(2,1)}, f32[36,36,2,128]{3,2,1,0:T(2,128)}, f32[36,36,2,128]{...) custom-call(bf16[2,2,5,2,9,16,128]{6,5,4,3,2,1,0:T(8,128)(2,1)S(1)} , ...), custom_call_target="tpu_custom_call" | custom-call | tf_op jit(solution)/shard_map/update/pallas_call | solution.py:375
  236.2 221.2 %all_gather.1.VO = bf16[6,2,2,4,9,2,9,16,128]{8,7,6,5,4,3,2,1,0:T(8,128)(2,1)S(1)} custom-call(bf16[4,5,2,9,16,128]{5,4,3,2,1,0:T(8,128)(2,1)} %get-tuple-element.32.wgu, bf16[2,9,9,16,128]{4,3,2,1,0:T(8,128)(2,1)} %get-tuple-element.33.wd), custom_call_target="tpu_custom_call" | custom-call | tf_op jit(solution)/shard_map/all_gather/pallas_call | solution.py:527
  457.5 20.2 %place.1 = (bf16[2,2,2,4,9,2,9,16,128]{8,7,6,5,4,3,2,1,0:T(8,128)(2,1)}, bf16[2,2,2,4,9,2,9,16,128]{8,7,6,5,4,3,2,1,0:T(8,128)(2,1)}, bf16[2,2,2,4,2,9,9,16,128]{8,7,6,5,4,3,2,1,0:T(8,128)(2,1)}) custom-call(bf16[6,2,2,4,9,2,9,16,128]{8,7,6,5,4,3,2,1,0:T(8,128)(2,1)S(1)} %all_gather.1.VO), custom_call_target="tpu_custom_call" | custom-call | tf_op jit(solution)/shard_map/place/pallas_call | solution.py:538
